TPU v7x, 32 devices: a 4x4x1 block of a 4x4x8 slice. The times are simulated.
32 devices in a mesh: rep: 1 (over z), data: 4 (over y), expert: 8 (over x, core).
Axes of the slice: x: 4, y: 4, z: 1, core: 2. Of those that a mesh axis runs over, the one named last changes fastest.
The devices are a block of a 4x4x8 slice.
Arguments:
- tok_in: bfloat16 [65536, 768], P(('rep', 'expert', 'data'))
- expert_idx: int32 [65536, 4], P(('rep', 'expert', 'data'))
- gate_wt: float32 [65536, 4], P(('rep', 'expert', 'data'))
- w_gate: bfloat16 [16, 768, 1344], P('expert', 'data')
- w_up: bfloat16 [16, 768, 1344], P('expert', 'data')
- w_down: bfloat16 [16, 1344, 768], P('expert', None, 'data')
- grad_out: bfloat16 [65536, 768], P(('rep', 'expert', 'data'))
Outputs:
- output 1: bfloat16 [65536, 768], P(('rep', 'expert', 'data'))
- output 2: bfloat16 [65536, 768], P(('rep', 'expert', 'data'))
- output 3: float32 [16, 768, 1344], P(('rep', 'expert'), 'data')
- output 4: float32 [16, 768, 1344], P(('rep', 'expert'), 'data')
- output 5: float32 [16, 1344, 768], P(('rep', 'expert'), None, 'data')
All inputs are finite; a program needn't handle non-finite values.
Results may differ from a plain program's by a relative error of at most 0.001.
Values are sent between devices in bfloat16 or wider.
A program may use at most 768 MiB of HBM per device.

v0:
```python
import jax
import jax.numpy as jnp
from jax import lax
from jax.sharding import PartitionSpec as P


def route_plan(pair_ids, block_expert, block_of_expert, capacity):
    pair_count = pair_ids.shape[0]
    n_exp = block_expert.shape[0]
    pair_order = jnp.argsort(pair_ids, stable=True)
    sorted_ids = jnp.take(pair_ids, pair_order)
    all_exp = jnp.arange(n_exp, dtype=pair_ids.dtype)
    exp_start = jnp.searchsorted(sorted_ids, all_exp, side="left")
    exp_end = jnp.searchsorted(sorted_ids, all_exp, side="right")
    pair_rank = jnp.argsort(pair_order, stable=True)
    pair_slot = pair_rank - jnp.take(exp_start, pair_ids)
    pair_dest = jnp.where(pair_slot < capacity, jnp.take(block_of_expert, pair_ids) * capacity + pair_slot, n_exp * capacity)
    seat_ids = jnp.arange(capacity)
    seat_start = jnp.take(exp_start, block_expert)[:, None] + seat_ids[None, :]
    seat_count = jnp.take(exp_end - exp_start, block_expert)[:, None]
    src_pair = jnp.where(seat_ids[None, :] < seat_count, jnp.take(pair_order, jnp.minimum(seat_start, pair_count - 1)), pair_count)
    return src_pair.reshape(-1), pair_dest


def gather_rows(table, index):
    return jnp.take(table, index, axis=0, mode="fill", fill_value=0)


def solution(mesh):
    ep_size = mesh.shape["expert"]
    row_spec = P(("rep", "expert", "data"), None)
    wide_spec = P("expert", "data", None)
    down_spec = P("expert", None, "data")
    wide_out = P(("rep", "expert"), "data", None)
    down_out = P(("rep", "expert"), None, "data")

    def local_step(tok_in, expert_idx, gate_wt, w_gate, w_up, w_down, grad_out):
        tokens, top_k = expert_idx.shape
        width = tok_in.shape[1]
        n_loc = w_gate.shape[0]
        n_exp = n_loc * ep_size
        capacity = (5 * top_k * tokens + 4 * n_exp - 1) // (4 * n_exp)
        loc_ids = jnp.arange(n_loc, dtype=jnp.int32)
        pos_ids = jnp.arange(ep_size, dtype=jnp.int32)
        block_expert = (pos_ids[None, :] * n_loc + loc_ids[:, None]).reshape(-1)
        all_exp = jnp.arange(n_exp, dtype=jnp.int32)
        block_of_expert = (all_exp % n_loc) * ep_size + all_exp // n_loc
        src_pair, pair_dest = route_plan(expert_idx.reshape(-1), block_expert, block_of_expert, capacity)
        src_tok = src_pair // top_k
        buf_shape = (n_loc, ep_size, capacity, width)

        send_rows = gather_rows(tok_in, src_tok).reshape(buf_shape)
        recv_rows = lax.all_to_all(send_rows, "expert", 1, 1, tiled=True)
        wg_full = lax.all_gather(w_gate, "data", axis=1, tiled=True)
        wu_full = lax.all_gather(w_up, "data", axis=1, tiled=True)
        wd_full = lax.all_gather(w_down, "data", axis=2, tiled=True)
        pre_gate = jnp.einsum("lscd,ldf->lscf", recv_rows, wg_full, preferred_element_type=jnp.float32)
        pre_up = jnp.einsum("lscd,ldf->lscf", recv_rows, wu_full, preferred_element_type=jnp.float32)
        sig_gate = jax.nn.sigmoid(pre_gate)
        silu_gate = pre_gate * sig_gate
        hid_act = (silu_gate * pre_up).astype(jnp.bfloat16)
        exp_out = jnp.einsum("lscf,lfd->lscd", hid_act, wd_full, preferred_element_type=jnp.float32).astype(jnp.bfloat16)
        back_out = lax.all_to_all(exp_out, "expert", 1, 1, tiled=True).reshape(-1, width)
        pair_out = gather_rows(back_out, pair_dest).reshape(tokens, top_k, width)
        tok_out = (tok_in.astype(jnp.float32) + jnp.sum(gate_wt[:, :, None] * pair_out.astype(jnp.float32), axis=1)).astype(jnp.bfloat16)

        gate_rows = gather_rows(gate_wt.reshape(-1), src_pair)
        dy_rows = gather_rows(grad_out, src_tok)
        send_cots = (gate_rows[:, None] * dy_rows.astype(jnp.float32)).astype(jnp.bfloat16).reshape(buf_shape)
        recv_cots = lax.all_to_all(send_cots, "expert", 1, 1, tiled=True)
        part_down = jnp.einsum("lscf,lscd->lfd", hid_act, recv_cots, preferred_element_type=jnp.float32)
        grad_hid = jnp.einsum("lscd,lfd->lscf", recv_cots, wd_full, preferred_element_type=jnp.float32)
        grad_pre_gate = (grad_hid * pre_up * sig_gate * (1.0 + pre_gate * (1.0 - sig_gate))).astype(jnp.bfloat16)
        grad_pre_up = (grad_hid * silu_gate).astype(jnp.bfloat16)
        part_gate = jnp.einsum("lscd,lscf->ldf", recv_rows, grad_pre_gate, preferred_element_type=jnp.float32)
        part_up = jnp.einsum("lscd,lscf->ldf", recv_rows, grad_pre_up, preferred_element_type=jnp.float32)
        grad_rows = (jnp.einsum("lscf,ldf->lscd", grad_pre_gate, wg_full, preferred_element_type=jnp.float32) + jnp.einsum("lscf,ldf->lscd", grad_pre_up, wu_full, preferred_element_type=jnp.float32)).astype(jnp.bfloat16)
        back_grad = lax.all_to_all(grad_rows, "expert", 1, 1, tiled=True).reshape(-1, width)
        pair_grad = gather_rows(back_grad, pair_dest).reshape(tokens, top_k, width)
        grad_in = (grad_out.astype(jnp.float32) + jnp.sum(pair_grad.astype(jnp.float32), axis=1)).astype(jnp.bfloat16)
        grad_gate = lax.psum_scatter(part_gate, "data", scatter_dimension=1, tiled=True)
        grad_up = lax.psum_scatter(part_up, "data", scatter_dimension=1, tiled=True)
        grad_down = lax.psum_scatter(part_down, "data", scatter_dimension=2, tiled=True)
        return tok_out, grad_in, grad_gate, grad_up, grad_down

    return jax.shard_map(local_step, mesh=mesh, in_specs=(row_spec, row_spec, row_spec, wide_spec, wide_spec, down_spec, row_spec), out_specs=(row_spec, row_spec, wide_out, wide_out, down_out), check_vma=False)
```

profile of v0, /device:TPU:97, one launch (start us, length us, event | category | flops | bytes accessed | tf_op | source)
XLA Modules:
  0.0 1389.9 jit_solution(15047955298752505054)
XLA Ops:
  7.3 1.1 copy.23
  9.1 6.8 sort.31
  15.9 45.5 %gather_fusion.2 = s32[8192]{0:T(1024)S(1)} fusion(s32[8192]{0:T(1024)S(1)} %reshape.245, s32[8192]{0:T(1024)S(1)} %fusion.42), kind=kCustom, calls=%fused_computation.8 | custom fusion | bytes 98304 | tf_op jit(solution)/shard_map/jit(_take)/gather | solution.py:11
  61.5 10.0 while.49
  61.5 0.7 gather_fusion.1
  62.3 0.7 gather_fusion.1
  63.0 0.7 gather_fusion.1
  63.7 0.7 gather_fusion.1
  64.4 0.7 gather_fusion.1
  65.1 0.7 gather_fusion.1
  65.8 0.7 gather_fusion.1
  66.5 0.7 gather_fusion.1
  71.5 10.0 while.48
  77.2 0.7 gather_fusion
  77.9 0.7 gather_fusion
  78.6 0.7 gather_fusion
  79.3 0.7 gather_fusion
  81.5 0.7 gather_fusion.5
  82.1 0.7 gather_fusion.6
  83.5 0.7 reshape.248
  84.4 56.8 %gather_fusion.3 = s32[10240]{0:T(1024)S(1)} fusion(s32[8192]{0:T(1024)S(1)} %get-tuple-element.141, s32[10240]{0:T(1024)S(1)} %broadcast_clamp_fusion.2), kind=kCustom, calls=%fused_computation.9 | custom fusion | bytes 122880 | tf_op jit(solution)/shard_map/jit(_take)/gather | solution.py:21
  141.5 56.8 %gather_fusion.4 = f32[10240]{0:T(1024)S(1)} fusion(f32[8192]{0:T(1024)S(1)} %reshape.248, s32[10240]{0:T(1024)S(1)} %broadcast_clamp_fusion.1), kind=kCustom, calls=%fused_computation.10 | custom fusion | bytes 122880 | tf_op jit(solution)/shard_map/jit(_take)/gather | solution.py:26
  198.4 42.9 %gather_fusion.7 = bf16[10240,768]{1,0:T(8,128)(2,1)} fusion(bf16[2048,768]{1,0:T(8,128)(2,1)S(1)} %copy-done.4, s32[10240]{0:T(1024)S(1)} %broadcast_clamp_fusion), kind=kCustom, calls=%fused_computation.3.clone | custom fusion | bytes 31498240 | tf_op jit(solution)/shard_map/jit(_take)/gather | solution.py:26
  241.3 10.0 broadcast_select_fusion.4
  251.2 6.4 copy.24
  257.6 7.8 all-to-all-start
  265.4 0.7 all-gather.6.cloned.1.call-update
  266.2 0.7 all-gather.4.cloned.1.call-update
  267.0 42.9 %gather_fusion.9 = bf16[10240,768]{1,0:T(8,128)(2,1)} fusion(bf16[2048,768]{1,0:T(8,128)(2,1)S(1)} %copy-done.6, s32[10240]{0:T(1024)S(1)} %broadcast_clamp_fusion), kind=kCustom, calls=%fused_computation.6.clone | custom fusion | bytes 31498240 | tf_op jit(solution)/shard_map/jit(_take)/gather | solution.py:26
  309.9 10.8 multiply_convert_fusion.3
  320.6 6.3 copy.30
  327.0 110.7 %all-to-all-done = bf16[2,8,640,768]{3,2,0,1:T(8,128)(2,1)} async-done(((bf16[2,8,640,768]{3,2,0,1:T(8,128)(2,1)}), bf16[2,8,640,768]{3,2,0,1:T(8,128)(2,1)}, u32[]{:S(2)}, u32[]{:S(2)}) %all-to-all-start) | async-done | bytes 15728672 | tf_op jit(solution)/shard_map/all_to_all | solution.py:53
  437.7 6.6 all-to-all-start.2
  444.3 0.7 all-gather.8.cloned.1.call-update
  445.4 31.6 %fusion.17 = f32[2,8,640,1344]{2,3,1,0:T(8,128)} fusion(bf16[2,8,640,768]{3,2,0,1:T(8,128)(2,1)} %all-to-all-done, bf16[2,768,1344]{2,1,0:T(8,128)(2,1)} %all-gather.6.cloned.1.call-done), kind=kOutput, calls=%fused_computation.44 | convolution fusion | flops 21139292160 | bytes 74907648 | tf_op jit(solution)/shard_map/lscd,ldf->lscf/dot_general | solution.py:58
  476.9 31.5 %fusion.19 = f32[2,8,640,1344]{2,3,1,0:T(8,128)} fusion(bf16[2,8,640,768]{3,2,0,1:T(8,128)(2,1)} %all-to-all-done, bf16[2,768,1344]{2,1,0:T(8,128)(2,1)} %all-gather.4.cloned.1.call-done), kind=kOutput, calls=%fused_computation.46 | convolution fusion | flops 21139292160 | bytes 74907648 | tf_op jit(solution)/shard_map/lscd,ldf->lscf/dot_general | solution.py:57
  508.5 108.1 %all-to-all-done.2 = bf16[2,8,640,768]{3,2,0,1:T(8,128)(2,1)} async-done(((bf16[2,8,640,768]{3,2,0,1:T(8,128)(2,1)}), bf16[2,8,640,768]{3,2,0,1:T(8,128)(2,1)}, u32[]{:S(2)}, u32[]{:S(2)}) %all-to-all-start.2) | async-done | bytes 15728672 | tf_op jit(solution)/shard_map/all_to_all | solution.py:70
  616.6 81.2 %multiply_convert_fusion = (bf16[2,8,640,1344]{2,3,1,0:T(8,128)(2,1)}, bf16[2,8,640,1344]{2,3,1,0:T(8,128)(2,1)}, bf16[2,8,640,1344]{2,3,1,0:T(8,128)(2,1)}) fusion(f32[2,8,640,1344]{2,3,1,0:T(8,128)} %fusion.19, f32[2,8,640,1344]{2,3,1,0:T(8,128)} %fusion.17, bf16[2,1344,768]{1,2,0:T(8,128)(2,1)} %all-gather.8.cloned.1.call-done, ...), kind=kOutput, calls=%fused_computation.27 | convolution fusion | flops 21345730560 | bytes 212533248 | tf_op jit(solution)/shard_map/lscd,lfd->lscf/dot_general | solution.py:72
  697.8 31.7 %fusion.21 = f32[2,1344,768]{1,2,0:T(8,128)} fusion(bf16[2,8,640,1344]{2,3,1,0:T(8,128)(2,1)} %get-tuple-element.205, bf16[2,8,640,768]{3,2,0,1:T(8,128)(2,1)} %all-to-all-done.2), kind=kOutput, calls=%fused_computation.53 | convolution fusion | flops 21139292160 | bytes 51511296 | tf_op jit(solution)/shard_map/lscf,lscd->lfd/dot_general | solution.py:71
  729.5 37.2 %fusion.32 = f32[2,8,640,768]{3,2,1,0:T(8,128)} fusion(bf16[2,8,640,1344]{2,3,1,0:T(8,128)(2,1)} %get-tuple-element.204, bf16[2,768,1344]{2,1,0:T(8,128)(2,1)} %all-gather.4.cloned.1.call-done), kind=kOutput, calls=%fused_computation.58 | convolution fusion | flops 21139292160 | bytes 63111168 | tf_op jit(solution)/shard_map/lscf,ldf->lscd/dot_general | solution.py:77
  766.7 37.1 %add_convert_fusion = bf16[2,8,640,768]{3,2,1,0:T(8,128)(2,1)} fusion(f32[2,8,640,768]{3,2,1,0:T(8,128)} %fusion.32, bf16[2,8,640,1344]{2,3,1,0:T(8,128)(2,1)} %get-tuple-element.203, bf16[2,768,1344]{2,1,0:T(8,128)(2,1)} %all-gather.6.cloned.1.call-done), kind=kOutput, calls=%fused_computation.32 | convolution fusion | flops 21155020800 | bytes 78839808 | tf_op jit(solution)/shard_map/lscf,ldf->lscd/dot_general | solution.py:77
  803.7 13.3 copy.32
  817.0 6.6 all-to-all-start.3
  823.6 35.8 %fusion.24 = f32[2,768,1344]{2,1,0:T(8,128)} fusion(bf16[2,8,640,768]{3,2,0,1:T(8,128)(2,1)} %all-to-all-done, bf16[2,8,640,1344]{2,3,1,0:T(8,128)(2,1)} %get-tuple-element.204), kind=kOutput, calls=%fused_computation.54 | convolution fusion | flops 21139292160 | bytes 51511296 | tf_op jit(solution)/shard_map/lscd,lscf->ldf/dot_general | solution.py:75
  859.4 36.1 %convolution_convert_fusion = bf16[2,8,640,768]{3,2,1,0:T(8,128)(2,1)} fusion(bf16[2,8,640,1344]{2,3,1,0:T(8,128)(2,1)} %get-tuple-element.205, bf16[2,1344,768]{1,2,0:T(8,128)(2,1)} %all-gather.8.cloned.1.call-done), kind=kOutput, calls=%fused_computation.48 | convolution fusion | flops 21147156480 | bytes 47382528 | tf_op jit(solution)/shard_map/lscf,lfd->lscd/dot_general | solution.py:62
  895.6 13.3 copy.27
  908.8 87.1 %all-to-all-done.3 = bf16[2,8,640,768]{3,2,0,1:T(8,128)(2,1)} async-done(((bf16[2,8,640,768]{3,2,0,1:T(8,128)(2,1)}), bf16[2,8,640,768]{3,2,0,1:T(8,128)(2,1)}, u32[]{:S(2)}, u32[]{:S(2)}) %all-to-all-start.3) | async-done | bytes 15728672 | tf_op jit(solution)/shard_map/all_to_all | solution.py:78
  995.9 6.6 all-to-all-start.1
  1002.5 35.7 %fusion.27 = f32[2,768,1344]{2,1,0:T(8,128)} fusion(bf16[2,8,640,768]{3,2,0,1:T(8,128)(2,1)} %all-to-all-done, bf16[2,8,640,1344]{2,3,1,0:T(8,128)(2,1)} %get-tuple-element.203), kind=kOutput, calls=%fused_computation.55 | convolution fusion | flops 21139292160 | bytes 51511296 | tf_op jit(solution)/shard_map/lscd,lscf->ldf/dot_general | solution.py:76
  1038.3 6.8 sort.32
  1045.1 0.7 fusion.46
  1045.8 0.7 fusion.47
  1046.5 20.3 %compare_and_fusion.1 = (pred[8192]{0:T(1024)(128)(4,1)S(1)}, s32[8192]{0:T(1024)S(1)}) fusion(s32[]{:T(128)} %bitcast.31, s32[]{:T(128)} %bitcast.30, s32[]{:T(128)} %bitcast.29, s32[]{:T(128)} %bitcast.28, s32[]{:T(128)} %bitcast.27, s32[]{:T(128)} %bitcast.26, s32[]{:T(128)} %bitcast.25, s32[]{:T(128)} %bitcast.24, s32[]{:T(128)} %bitcast.23, ...), kind=kLoop, calls=%fused_computation.90 | loop fusion | flops 524288 | bytes 106624 | tf_op jit(solution)/shard_map/jit(_take)/and | solution.py:26
  1066.8 13.3 copy.33
  1080.1 44.6 %gather_fusion.10 = bf16[8192,768]{1,0:T(8,128)(2,1)} fusion(bf16[10240,768]{1,0:T(8,128)(2,1)} %bitcast.97, s32[8192]{0:T(1024)S(1)} %broadcast_clamp_fusion.3), kind=kCustom, calls=%fused_computation.7.clone | custom fusion | bytes 25198592 | tf_op jit(solution)/shard_map/jit(_take)/gather | solution.py:26
  1124.7 50.0 %all-to-all-done.1 = bf16[2,8,640,768]{3,2,0,1:T(8,128)(2,1)} async-done(((bf16[2,8,640,768]{3,2,0,1:T(8,128)(2,1)}), bf16[2,8,640,768]{3,2,0,1:T(8,128)(2,1)}, u32[]{:S(2)}, u32[]{:S(2)}) %all-to-all-start.1) | async-done | bytes 15728672 | tf_op jit(solution)/shard_map/all_to_all | solution.py:63
  1174.7 13.2 copy.28
  1187.9 44.5 %gather_fusion.8 = bf16[8192,768]{1,0:T(8,128)(2,1)} fusion(bf16[10240,768]{1,0:T(8,128)(2,1)} %bitcast.96, s32[8192]{0:T(1024)S(1)} %broadcast_clamp_fusion.3), kind=kCustom, calls=%fused_computation.4.clone | custom fusion | bytes 25198592 | tf_op jit(solution)/shard_map/jit(_take)/gather | solution.py:26
  1232.4 25.0 %select_convert_fusion = (f32[8192,768]{1,0:T(8,128)}, f32[8192,768]{1,0:T(8,128)}) fusion(bf16[8192,768]{1,0:T(8,128)(2,1)} %gather_fusion.10, pred[8192]{0:T(1024)(128)(4,1)S(1)} %get-tuple-element.197, bf16[8192,768]{1,0:T(8,128)(2,1)} %gather_fusion.8), kind=kLoop, calls=%fused_computation.49 | loop fusion | flops 25165824 | bytes 75505664 | tf_op jit(solution)/shard_map/convert_element_type | solution.py:80
  1257.4 28.6 %reshape.252 = f32[2048,4,768]{2,1,0:T(4,128)} reshape(f32[8192,768]{1,0:T(8,128)} %get-tuple-element.206) | data formatting | bytes 50331648 | tf_op jit(solution)/shard_map/convert_element_type | solution.py:80
  1285.9 28.5 %reshape.251 = f32[2048,4,768]{2,1,0:T(4,128)} reshape(f32[8192,768]{1,0:T(8,128)} %get-tuple-element.207) | data formatting | bytes 50331648 | tf_op jit(solution)/shard_map/convert_element_type | solution.py:65
  1314.5 36.9 %reduce_sum.19 = f32[2048,768]{1,0:T(8,128)} reduce(f32[2048,4,768]{2,1,0:T(4,128)} %reshape.252, f32[]{:T(128)} %constant.190.clone.1), dimensions={1}, to_apply=%region_7.12 | reduce | flops 4718592 | bytes 31457284 | tf_op jit(solution)/shard_map/reduce_sum | solution.py:80
  1351.3 21.6 %multiply_reduce_fusion = f32[2048,768]{1,0:T(8,128)} fusion(f32[2048,4,768]{2,1,0:T(4,128)} %reshape.251, f32[2048,4]{1,0:T(8,128)} %copy-done.9), kind=kLoop, calls=%fused_computation.38 | loop fusion | flops 11010048 | bytes 31490048 | tf_op jit(solution)/shard_map/reduce_sum | solution.py:65
  1372.9 9.6 add_convert_fusion.1
  (176 shorter events, 13.9 us)
Async XLA Ops:
  9.1 52.4 %copy-start.2 = (s32[8192]{0:T(1024)}, s32[8192]{0:T(1024)S(1)}, u32[]{:S(2)}) copy-start(s32[8192]{0:T(1024)S(1)} %reshape.245) | copy-start | bytes 98308
  15.9 68.5 %copy-start = (s32[8192]{0:T(1024)}, s32[8192]{0:T(1024)S(1)}, u32[]{:S(2)}) copy-start(s32[8192]{0:T(1024)S(1)} %get-tuple-element.141) | copy-start | bytes 98308
  15.9 67.1 %copy-start.10 = (f32[2048,4]{0,1:T(4,128)S(1)}, f32[2048,4]{0,1:T(4,128)}, u32[]{:S(2)}) copy-start(f32[2048,4]{0,1:T(4,128)} %param.21) | copy-start | bytes 98308
  81.5 1.6 copy-start.7
  83.4 57.7 %copy-start.9 = (f32[2048,4]{1,0:T(8,128)}, f32[2048,4]{1,0:T(8,128)S(1)}, u32[]{:S(2)}) copy-start(f32[2048,4]{1,0:T(8,128)S(1)} %copy.22) | copy-start | bytes 98308
  141.5 56.9 %copy-start.4 = (bf16[2048,768]{1,0:T(8,128)(2,1)S(1)}, bf16[2048,768]{1,0:T(8,128)(2,1)}, u32[]{:S(2)}) copy-start(bf16[2048,768]{1,0:T(8,128)(2,1)} %param.19) | copy-start | bytes 9437188
  257.6 9.4 copy-start.6
  257.6 180.1 %all-to-all-start = ((bf16[2,8,640,768]{3,2,0,1:T(8,128)(2,1)}), bf16[2,8,640,768]{3,2,0,1:T(8,128)(2,1)}, u32[]{:S(2)}, u32[]{:S(2)}) async-start(bf16[2,8,640,768]{3,2,0,1:T(8,128)(2,1)} %copy.24), calls=%async_computation | async-start | bytes 31457280 | tf_op jit(solution)/shard_map/all_to_all | solution.py:53
  265.4 179.9 %all-gather.6.cloned.1.call-start = ((), (), s32[]{:S(2)}) async-start(), calls=%async_computation.8 | async-start | bytes 5406720 | tf_op jit(solution)/shard_map/all_gather | solution.py:55
  266.2 210.8 %all-gather.4.cloned.1.call-start = ((), (), s32[]{:S(2)}) async-start(), calls=%async_computation.7 | async-start | bytes 5406720 | tf_op jit(solution)/shard_map/all_gather | solution.py:54
  437.7 178.9 %all-to-all-start.2 = ((bf16[2,8,640,768]{3,2,0,1:T(8,128)(2,1)}), bf16[2,8,640,768]{3,2,0,1:T(8,128)(2,1)}, u32[]{:S(2)}, u32[]{:S(2)}) async-start(bf16[2,8,640,768]{3,2,0,1:T(8,128)(2,1)} %copy.30), calls=%async_computation.2 | async-start | bytes 31457280 | tf_op jit(solution)/shard_map/all_to_all | solution.py:70
  444.3 64.2 %all-gather.8.cloned.1.call-start = ((), (), s32[]{:S(2)}) async-start(), calls=%async_computation.9 | async-start | bytes 5406720 | tf_op jit(solution)/shard_map/all_gather | solution.py:56
  445.1 937.5 %reduce-scatter.8.cloned.1.call-start = ((), (), s32[]{:S(2)}) async-start(), calls=%async_computation.12 | async-start | bytes 10813440 | tf_op jit(solution)/shard_map/reduce_scatter | solution.py:83
  817.0 178.9 %all-to-all-start.3 = ((bf16[2,8,640,768]{3,2,0,1:T(8,128)(2,1)}), bf16[2,8,640,768]{3,2,0,1:T(8,128)(2,1)}, u32[]{:S(2)}, u32[]{:S(2)}) async-start(bf16[2,8,640,768]{3,2,0,1:T(8,128)(2,1)} %copy.32), calls=%async_computation.3 | async-start | bytes 31457280 | tf_op jit(solution)/shard_map/all_to_all | solution.py:78
  823.6 558.9 %reduce-scatter.4.cloned.1.call-start = ((), (), s32[]{:S(2)}) async-start(), calls=%async_computation.10 | async-start | bytes 10813440 | tf_op jit(solution)/shard_map/reduce_scatter | solution.py:81
  995.9 178.8 %all-to-all-start.1 = ((bf16[2,8,640,768]{3,2,0,1:T(8,128)(2,1)}), bf16[2,8,640,768]{3,2,0,1:T(8,128)(2,1)}, u32[]{:S(2)}, u32[]{:S(2)}) async-start(bf16[2,8,640,768]{3,2,0,1:T(8,128)(2,1)} %copy.27), calls=%async_computation.1 | async-start | bytes 31457280 | tf_op jit(solution)/shard_map/all_to_all | solution.py:63
  1002.4 35.8 %copy-start.1 = (s32[8192]{0:T(1024)S(1)}, s32[8192]{0:T(1024)}, u32[]{:S(2)}) copy-start(s32[8192]{0:T(1024)} %copy-done) | copy-start | bytes 98308
  1002.4 42.6 %copy-start.8 = (s32[16]{0:T(128)S(1)}, s32[16]{0:T(128)}, u32[]{:S(2)}) copy-start(s32[16]{0:T(128)} %copy-done.7) | copy-start | bytes 196
  1002.4 44.1 %copy-start.3 = (s32[8192]{0:T(1024)S(1)}, s32[8192]{0:T(1024)}, u32[]{:S(2)}) copy-start(s32[8192]{0:T(1024)} %copy-done.2) | copy-start | bytes 98308
  1002.4 380.1 %reduce-scatter.6.cloned.1.call-start = ((), (), s32[]{:S(2)}) async-start(), calls=%async_computation.11 | async-start | bytes 10813440 | tf_op jit(solution)/shard_map/reduce_scatter | solution.py:82
  1351.3 21.6 %copy-start.5 = (bf16[2048,768]{1,0:T(8,128)(2,1)S(1)}, bf16[2048,768]{1,0:T(8,128)(2,1)}, u32[]{:S(2)}) copy-start(bf16[2048,768]{1,0:T(8,128)(2,1)} %param.19) | copy-start | bytes 9437188
Sparse Core Ops, SparseCore 0:
  267.8 48.5 all-gather.5
  318.0 47.0 all-gather.3
  446.7 48.5 all-gather.7
  729.6 80.7 reduce-scatter.7
  859.6 82.0 reduce-scatter.3
  1038.4 82.1 reduce-scatter.5
where the time goes:
time: 1400 us; the launch traced here: 1390 us
  local copies, waits for them, and re-layouts  481 us (34%)
  waiting for transfers between devices  358 us (26%)
  matrix products  358 us (26%)
  other arithmetic  149 us (11%)
  starting transfers between devices  28 us (2%)
  between operations  15 us (1%)
    gather x5, local copies, waits for them, and re-layouts, gather_rows(): return jnp.take(table, index, axis=0, mode='fill', fill_value=0)  232 us
    all_to_all x1, waiting for transfers between devices, local_step(): recv_rows = lax.all_to_all(send_rows, 'expert', 1, 1, tiled=True)  111 us
    all_to_all x1, waiting for transfers between devices, local_step(): recv_cots = lax.all_to_all(send_cots, 'expert', 1, 1, tiled=True)  108 us
    all_to_all x1, waiting for transfers between devices, local_step(): lax.all_to_all(grad_rows, 'expert', 1, 1, tiled=True).reshape(-1, width)  87.1 us
    dot_general x1, matrix products, local_step(): jnp.einsum('lscd,lfd->lscf', recv_cots, wd_full, preferred_element_type=j...  81.2 us
    gather x1, local copies, waits for them, and re-layouts, route_plan(): jnp.take(pair_order, jnp.minimum(seat_start, pair_count - 1))  56.8 us
    all_to_all x1, waiting for transfers between devices, local_step(): lax.all_to_all(exp_out, 'expert', 1, 1, tiled=True).reshape(-1, width)  50 us
    gather x1, local copies, waits for them, and re-layouts, route_plan(): sorted_ids = jnp.take(pair_ids, pair_order)  45.5 us
  transfers between devices with their start and end apart: 10, of which 4 were waited for; matrix products, arithmetic and copies ran while one was open for 45% of the time, Pallas kernels for 0%

commit v1 on v0

v1 whole, which is shorter than its diff:
```python
import functools

import jax
import jax.numpy as jnp
from jax import lax
from jax.experimental import pallas as pl
from jax.experimental.pallas import tpu as pltpu
from jax.sharding import PartitionSpec as P


BF = jnp.bfloat16
F32 = jnp.float32
ANY = pl.ANY

RELATION = ((0, 0), (0, 1), (1, 0), (1, 1), (-1, 0), (-1, 1), (2, 0), (2, 1))
BLK, WIN = 256, 272
CBLK, CWIN = 128, 144


def nn(lhs, rhs):
    return jnp.dot(lhs, rhs, preferred_element_type=F32)


def nt(lhs, rhs):
    return lax.dot_general(lhs, rhs, (((1,), (1,)), ((), ())), preferred_element_type=F32)


def tn(lhs, rhs):
    return lax.dot_general(lhs, rhs, (((0,), (0,)), ((), ())), preferred_element_type=F32)


def params():
    return pltpu.CompilerParams(vmem_limit_bytes=62 * 2**20, dimension_semantics=("arbitrary",))


def cost(flops, moved):
    return pl.CostEstimate(flops=int(flops), bytes_accessed=int(moved), transcendentals=0)


def route_kernel(capacity, idx_ref, gate_ref, eid_ref, out_ref, col_ref):
    n_exp, tokens = eid_ref.shape[0], idx_ref.shape[1]
    eid = eid_ref[...]
    hit = jnp.zeros((n_exp, tokens), F32)
    gate = jnp.zeros((n_exp, tokens), F32)
    for j in range(idx_ref.shape[0]):
        same = idx_ref[j:j + 1, :] == eid
        hit = jnp.where(same, 1.0, hit)
        gate = jnp.where(same, gate_ref[j:j + 1, :], gate)
    before = (lax.broadcasted_iota(jnp.int32, (128, 128), 0) < lax.broadcasted_iota(jnp.int32, (128, 128), 1)).astype(F32).astype(BF)
    seen = jnp.zeros((n_exp, 1), F32)
    for b in range(tokens // 128):
        h = hit[:, b * 128:(b + 1) * 128]
        slot = nn(h.astype(BF), before) + seen
        seen = seen + jnp.sum(h, axis=1, keepdims=True)
        pos = jnp.where((h > 0.0) & (slot < capacity), slot, -1.0)
        out_ref[:, 0, b * 128:(b + 1) * 128] = pos
        col_ref[b * 128:(b + 1) * 128, 0:n_exp] = pos.T
    out_ref[:, 1, :] = gate
    col_ref[:, n_exp:2 * n_exp] = gate.T


def route(idx_t, gate_t, eid, capacity):
    n_exp, tokens = eid.shape[0], idx_t.shape[1]
    return pl.pallas_call(
        functools.partial(route_kernel, capacity),
        out_shape=[jax.ShapeDtypeStruct((n_exp, 2, tokens), F32), jax.ShapeDtypeStruct((tokens, 2 * n_exp), F32)],
        cost_estimate=cost(20_000_000, 1_000_000), name="route",
    )(idx_t, gate_t, eid)


def choose(index, items, act):
    if len(items) == 1:
        act(items[0])
        return
    mid = len(items) // 2

    @pl.when(index < mid)
    def _():
        choose(index, items[:mid], act)

    @pl.when(index >= mid)
    def _():
        choose(index - mid, items[mid:], act)


def fetch_rows(tables, buf, sem, src, slot):
    def start(parts):
        row = 0
        for part in parts:
            pltpu.make_async_copy(part, buf.at[slot, pl.ds(row, part.shape[0])], sem.at[slot]).start()
            row += part.shape[0]

    choose(src, tables, start)


def await_rows(tables, buf, sem, slot):
    row = 0
    for part in tables[0]:
        pltpu.make_async_copy(part, buf.at[slot, pl.ds(row, part.shape[0])], sem.at[slot]).wait()
        row += part.shape[0]


def stage_rows(tables, buf, sem, source):
    step = pl.program_id(0)

    @pl.when(step == 0)
    def _():
        fetch_rows(tables, buf, sem, source(0), 0)

    @pl.when(step + 1 < pl.num_programs(0))
    def _():
        fetch_rows(tables, buf, sem, source(step + 1), (step + 1) % 2)

    await_rows(tables, buf, sem, step % 2)
    return step % 2


def gather_seats(posg_ref, base_ref, at, rows_ref, acc, gacc=None):
    acc[...] = jnp.zeros_like(acc)
    if gacc is not None:
        gacc[...] = jnp.zeros_like(gacc)
    iota = lax.broadcasted_iota(jnp.int32, (WIN, 1), 0).astype(F32)
    blocks = rows_ref.shape[0] // BLK
    for blk in range(blocks):
        base = pl.multiple_of(base_ref[at * blocks + blk], 8)
        cols = pl.ds(blk * BLK, BLK)
        hot = (posg_ref[0:1, cols] - base.astype(F32)) == iota
        win = pl.ds(base, WIN)
        acc[win, :] += nn(jnp.where(hot, 1.0, 0.0).astype(BF), rows_ref[cols, :])
        if gacc is not None:
            gacc[win, :] += jnp.sum(jnp.where(hot, posg_ref[1:2, cols], 0.0), axis=1, keepdims=True)


def split_refs(refs, sizes):
    out, at = [], 0
    for n in sizes:
        out.append(refs[at:at + n])
        at += n
    return out


def put(buf, slot, dests, sem, which):
    choose(which, dests, lambda dest: pltpu.make_async_copy(buf.at[slot], dest, sem.at[slot]).start())


def await_put(buf, slot, dests, sem):
    pltpu.make_async_copy(buf.at[slot], dests[0], sem.at[slot]).wait()


def fwd_kernel(sizes, n_w, n_skip, item, first_src, base_ref, *refs):
    n_tab, n_out = sum(sizes), len(sizes)
    tables = split_refs(refs[:n_tab], sizes)
    w_refs = refs[n_tab:n_tab + n_w]
    posg_ref = refs[n_tab + n_w + n_skip]
    rest = refs[n_tab + n_w + n_skip + 1:]
    outs = rest[:n_out]
    r_ref, h_ref, us_ref, buf, acc, ab, w, obuf, sem, osem, wsem = rest[n_out:]
    step, last = pl.program_id(0), pl.num_programs(0) - 1
    fp = h_ref.shape[1]
    n_loc = outs[0].shape[0]
    loc, src = item(step)
    w_at = loc if n_w > 1 else 0
    w_copies = [pltpu.make_async_copy(w_refs[i], w.at[i], wsem.at[i]) for i in range(n_w)]

    @pl.when(step == 0)
    def _():
        for copy in w_copies:
            copy.start()

    slot = stage_rows(tables, buf, sem, lambda s: item(s)[1] - first_src)
    gather_seats(posg_ref, base_ref, src * n_loc + loc, buf.at[slot], acc)
    r_ref[...] = acc[...].astype(BF)

    @pl.when(step == 0)
    def _():
        for copy in w_copies:
            copy.wait()

    @pl.when(step >= 2)
    def _():
        await_put(obuf, slot, [outs[0].at[0]], osem)

    ab[...] = nn(r_ref[...], w[w_at, :, :2 * fp])
    a = ab[:, :fp]
    b = ab[:, fp:]
    sg = jax.nn.sigmoid(a)
    silu = a * sg
    h_ref[...] = (silu * b).astype(BF)
    us_ref[:, :fp] = b * sg * (1.0 + a * (1.0 - sg))
    us_ref[:, fp:] = silu
    obuf[slot] = nt(h_ref[...], w[w_at, :, 2 * fp:]).astype(BF)
    put(obuf, slot, [out.at[loc] for out in outs], osem, src - first_src)

    @pl.when(step == last)
    def _():
        await_put(obuf, 1 - slot, [outs[0].at[0]], osem)
        await_put(obuf, slot, [outs[0].at[0]], osem)


def run_fwd(num, item, sources, base, tables, posg, ws, cap, outs=(), kept=()):
    n_src, n_loc, _, tokens = posg.shape
    width, wide = ws[0].shape
    fp = wide // 3
    any_spec = pl.BlockSpec(memory_space=ANY)
    tabs = tables[sources[0]:sources[1]]
    flat = [t for ts in tabs for t in ts]
    skip = (*outs, *kept)
    seat = lambda n: pl.BlockSpec((None, None, cap, n), lambda s, b: (*item(s), 0, 0))
    n_out = sources[1] - sources[0]
    n_in = 1 + len(flat) + len(ws)
    alias = {n_in + i: i for i in range(len(outs))} | {n_in + len(outs) + i: n_out + i for i in range(len(kept))}
    kept_shape = [jax.ShapeDtypeStruct((n_loc, n_src, cap, n), t) for n, t in ((width, BF), (fp, BF), (2 * fp, F32))]
    got = pl.pallas_call(
        functools.partial(fwd_kernel, tuple(len(ts) for ts in tabs), len(ws), len(skip), item, sources[0]),
        grid_spec=pltpu.PrefetchScalarGridSpec(
            num_scalar_prefetch=1, grid=(num,),
            in_specs=[any_spec] * (len(flat) + len(ws) + len(skip)) + [
                pl.BlockSpec((None, None, 2, tokens), lambda s, b: (*item(s)[::-1], 0, 0))],
            out_specs=[any_spec] * n_out + [seat(width), seat(fp), seat(2 * fp)],
            scratch_shapes=[pltpu.VMEM((2, tokens, width), BF), pltpu.VMEM((cap, width), F32), pltpu.VMEM((cap, 2 * fp), F32),
                            pltpu.VMEM((len(ws), width, wide), BF), pltpu.VMEM((2, cap, width), BF),
                            pltpu.SemaphoreType.DMA((2,)), pltpu.SemaphoreType.DMA((2,)), pltpu.SemaphoreType.DMA((len(ws),))]),
        out_shape=[jax.ShapeDtypeStruct((n_loc, cap, width), BF)] * n_out + kept_shape,
        input_output_aliases=alias,
        compiler_params=params(),
        cost_estimate=cost(2 * num * cap * width * wide, 12_000_000 * num),
    )(base, *flat, *ws, *skip, posg)
    return got[:n_out], got[n_out:]


def bwd_kernel(sizes, n_after, ffn, loc, n_loc, base_ref, *refs):
    n_tab, n_src = sum(sizes), len(sizes)
    tables = split_refs(refs[:n_tab], sizes)
    posg_ref, w_ref, r_ref, h_ref, us_ref = refs[n_tab + n_after:n_tab + n_after + 5]
    rest = refs[n_tab + n_after + 5:]
    outs = rest[:n_src]
    dw_ref, buf, gacc, dh, r2, c2, h2, dab2, dw, stage, obuf, sem, osem, rsem, dsem = rest[n_src:]
    step = pl.program_id(0)
    cap, fp = dh.shape
    width = c2.shape[1]
    rows = cap // 2
    slot = stage_rows(tables, buf, sem, lambda s: s)
    now = pl.multiple_of(slot * cap, cap)
    copies = [pltpu.make_async_copy(r_ref.at[loc, step], r2.at[pl.ds(now, cap)], rsem.at[0]),
              pltpu.make_async_copy(h_ref.at[loc, step], h2.at[pl.ds(now, cap)], rsem.at[1])]
    for copy in copies:
        copy.start()

    @pl.when(step == 0)
    def _():
        dw[...] = jnp.zeros_like(dw)

    gather_seats(posg_ref, base_ref, step * n_loc + loc, buf.at[slot], dh.at[:, pl.ds(0, width)], gacc)
    c2[pl.ds(now, cap), :] = (gacc[...] * dh[:, :width]).astype(BF)

    @pl.when(step >= 2)
    def _():
        await_put(obuf, slot, [outs[0].at[0]], osem)

    for half in range(2):
        part = pl.ds(half * rows, rows)
        here = pl.ds(pl.multiple_of(now + half * rows, rows), rows)
        dh[part, :] = nn(c2[here, :], w_ref[:, 2 * fp:])
        dab2[here, :fp] = (dh[part, :] * us_ref[part, :fp]).astype(BF)
        dab2[here, fp:] = (dh[part, :] * us_ref[part, fp:]).astype(BF)
        obuf[slot, part, :] = nt(dab2[here, :], w_ref[:, :2 * fp]).astype(BF)
    put(obuf, slot, [out.at[0] for out in outs], osem, step)
    for copy in copies:
        copy.wait()

    @pl.when(slot == 1)
    def _():
        dw[:, 2 * fp:] += tn(c2[...], h2[...])
        dw[:, :2 * fp] += tn(r2[...], dab2[...])

    @pl.when(step == n_src - 1)
    def _():
        await_put(obuf, 0, [outs[0].at[0]], osem)
        await_put(obuf, 1, [outs[0].at[0]], osem)
        flush = stage.shape[1]
        copies = []
        for i in range(3):
            for at_row in range(0, dw.shape[0], flush):
                use = len(copies) % 2
                if len(copies) >= 2:
                    copies[-2].wait()
                stage[use] = dw[at_row:at_row + flush, i * fp:i * fp + ffn]
                copies.append(pltpu.make_async_copy(stage.at[use], dw_ref.at[i, pl.ds(at_row, flush)], dsem.at[use]))
                copies[-1].start()
        for copy in copies[-2:]:
            copy.wait()


def run_bwd(loc, base, tables, posg, w, kept, cap, ffn, after=()):
    n_src, n_loc, _, tokens = posg.shape
    width, wide = w.shape
    fp = wide // 3
    flat = [t for ts in tables for t in ts]
    any_spec = pl.BlockSpec(memory_space=ANY)
    got = pl.pallas_call(
        functools.partial(bwd_kernel, tuple(len(ts) for ts in tables), len(after), ffn, loc, n_loc),
        grid_spec=pltpu.PrefetchScalarGridSpec(
            num_scalar_prefetch=1, grid=(n_src,),
            in_specs=[any_spec] * (len(flat) + len(after)) + [
                pl.BlockSpec((None, None, 2, tokens), lambda s, b: (s, loc, 0, 0)),
                pl.BlockSpec((width, wide), lambda s, b: (0, 0), pipeline_mode=pl.Buffered(1)),
                any_spec, any_spec,
                pl.BlockSpec((None, None, cap, 2 * fp), lambda s, b: (loc, s, 0, 0))],
            out_specs=[any_spec] * (n_src + 1),
            scratch_shapes=[pltpu.VMEM((2, tokens, width), BF), pltpu.VMEM((cap, 1), F32), pltpu.VMEM((cap, fp), F32),
                            pltpu.VMEM((2 * cap, width), BF), pltpu.VMEM((2 * cap, width), BF), pltpu.VMEM((2 * cap, fp), BF), pltpu.VMEM((2 * cap, 2 * fp), BF),
                            pltpu.VMEM((width, wide), F32), pltpu.VMEM((2, width // 6, ffn), F32), pltpu.VMEM((2, cap, width), BF),
                            pltpu.SemaphoreType.DMA((2,)), pltpu.SemaphoreType.DMA((2,)), pltpu.SemaphoreType.DMA((2,)), pltpu.SemaphoreType.DMA((2,))]),
        out_shape=[jax.ShapeDtypeStruct((1, cap, width), BF)] * n_src + [jax.ShapeDtypeStruct((3, width, ffn), F32)],
        compiler_params=pltpu.CompilerParams(vmem_limit_bytes=67_043_328, dimension_semantics=("arbitrary",)),
        cost_estimate=cost(4 * n_src * cap * width * wide, 12_000_000 * n_src),
    )(base, *flat, *after, posg, w, *kept)
    return got[:n_src], got[n_src]


def combine_kernel(cols, n_back, gated, n_after, per, base_ref, *refs):
    n = n_back
    back = refs[:n]
    start_ref, col_ref, out_ref, buf, sem = refs[n + n_after:]
    per_back, _, _ = back[0].shape
    step = pl.program_id(0)
    blocks = pl.num_programs(0) * per
    n_exp = col_ref.shape[1] // 2
    copies = [pltpu.make_async_copy(back[i], buf.at[pl.ds(i * per_back, per_back)], sem.at[i]) for i in range(n)]

    @pl.when(step == 0)
    def _():
        for copy in copies:
            copy.start()
        for copy in copies:
            copy.wait()

    iota = lax.broadcasted_iota(jnp.int32, (1, CWIN), 1).astype(F32)
    for b in range(per):
        rows_at = pl.ds(b * CBLK, CBLK)
        summed = None
        for i, col in enumerate(cols):
            base = pl.multiple_of(base_ref[col * blocks + step * per + b], 16)
            pick = jnp.where((col_ref[rows_at, col:col + 1] - base.astype(F32)) == iota, 1.0, 0.0).astype(BF)
            rows = nn(pick, buf[i, pl.ds(base, CWIN), :])
            if gated:
                rows = col_ref[rows_at, n_exp + col:n_exp + col + 1] * rows
            summed = rows if summed is None else summed + rows
        out_ref[rows_at, :] = (start_ref[rows_at, :].astype(F32) + summed).astype(out_ref.dtype)


def run_combine(back, cols, gated, start, col, base, dtype, after=(), per=4):
    _, cap, width = back[0].shape
    tokens, n = start.shape[0], len(back)
    spec = lambda w: pl.BlockSpec((per * CBLK, w), lambda s, b: (s, 0))
    any_spec = pl.BlockSpec(memory_space=ANY)
    return pl.pallas_call(
        functools.partial(combine_kernel, tuple(cols), n, gated, len(after), per),
        grid_spec=pltpu.PrefetchScalarGridSpec(
            num_scalar_prefetch=1, grid=(tokens // (per * CBLK),),
            in_specs=[any_spec] * (n + len(after)) + [spec(width), spec(col.shape[1])],
            out_specs=spec(width),
            scratch_shapes=[pltpu.VMEM((len(cols), cap, width), BF), pltpu.SemaphoreType.DMA((n,))]),
        out_shape=jax.ShapeDtypeStruct((tokens, width), dtype),
        compiler_params=params(), cost_estimate=cost(2 * len(cols) * tokens * 256 * width, 20_000_000),
    )(base, *back, *after, start, col)


def block_base(pos, block, window, cap, align):
    first = jnp.min(jnp.where(pos >= 0.0, pos, float(cap)).reshape(*pos.shape[:-1], -1, block), axis=-1)
    return (jnp.minimum(first.astype(jnp.int32), cap - window) // align * align).reshape(-1)


def solution(mesh):
    ep_size = mesh.shape["expert"]
    chips = ep_size // 2
    row_spec = P(("rep", "expert", "data"), None)
    wide_spec = P("expert", "data", None)
    down_spec = P("expert", None, "data")
    wide_out = P(("rep", "expert"), "data", None)
    down_out = P(("rep", "expert"), None, "data")

    def shift(v, steps, flip):
        return lax.ppermute(v, "expert", [(2 * c + k, 2 * ((c + steps) % chips) + (k ^ flip)) for c in range(chips) for k in range(2)])

    def tables(rows):
        half = rows.shape[0] // 2
        top, bottom = rows[:half], rows[half:]
        right_top, left_bottom = shift(top, 1, 0), shift(bottom, -1, 0)
        right_bottom, left_top = shift(bottom, 1, 0), shift(top, -1, 0)
        far = shift(right_top, 1, 0), shift(left_bottom, -1, 0)
        same = [(rows,), (right_top, right_bottom), (left_top, left_bottom), far]
        return [v for parts in same for v in (parts, tuple(shift(p, 0, 1) for p in parts))]

    def moe_step(tok_in, expert_idx, gate_wt, w_gate, w_up, w_down, grad_out):
        tokens, top_k = expert_idx.shape
        n_loc, _, ffn = w_gate.shape
        n_exp = n_loc * ep_size
        cap = (5 * top_k * tokens + 4 * n_exp - 1) // (4 * n_exp)
        n_src = len(RELATION)
        pad = (-ffn) % 128

        x_tabs = tables(tok_in)
        g_tabs = tables(grad_out)
        weights = []
        for e in range(n_loc):
            parts = [jnp.pad(v, ((0, 0), (0, pad))) for v in (w_gate[e], w_up[e], w_down[e].T)]
            packed = jnp.concatenate(parts, axis=1)
            weights.append(lax.all_gather(packed, "data", axis=0, tiled=True))

        me = lax.axis_index("expert")
        peers = jnp.stack([2 * ((me // 2 + s) % chips) + (me % 2 + f) % 2 for s, f in RELATION])
        eid = (peers[:, None] * n_loc + jnp.arange(n_loc)[None, :]).reshape(-1, 1).astype(jnp.int32)
        posg, col = route(expert_idx.T, gate_wt.T, eid, cap)
        home_base = block_base(posg[:, 0], CBLK, CWIN, cap, 16)
        posg = posg.reshape(n_src, n_loc, 2, tokens)
        moved = [posg[k] if k == 0 else shift(posg[k], *RELATION[k]) for k in range(n_src)]
        posg_in = jnp.stack(moved)
        base = block_base(posg_in[:, :, 0], BLK, WIN, cap, 8)

        def give_back(rows):
            return [rows[k] if k == 0 else shift(rows[k], -s, f) for k, (s, f) in enumerate(RELATION)]

        cut = n_src - 2
        outs, kept = run_fwd(cut, lambda s: (0, s), (0, cut), base, x_tabs, posg_in, weights[:1], cap)
        later = lambda s: (jnp.where(s < 2, 0, 1), jnp.where(s < 2, s + cut, s - 2))
        outs, kept = run_fwd(n_src + 2, later, (0, n_src), base, x_tabs, posg_in, weights, cap, outs, kept)
        back_o = give_back(outs)
        dr0, dw0 = run_bwd(0, base, g_tabs, posg_in, weights[0], kept, cap, ffn)
        back_d0 = give_back(dr0)
        g0 = lax.psum_scatter(dw0, "data", scatter_dimension=1, tiled=True)
        dr1, dw1 = run_bwd(1, base, g_tabs, posg_in, weights[1], kept, cap, ffn, after=(dw0,))
        back_d1 = give_back(dr1)
        g1 = lax.psum_scatter(dw1, "data", scatter_dimension=1, tiled=True)

        cols = [[k * n_loc + e for k in range(n_src)] for e in range(n_loc)]
        tok_out = run_combine(back_o, list(range(n_loc * n_src)), True, tok_in, col, home_base, BF, after=(dw1,))
        part = run_combine(back_d0, cols[0], False, grad_out, col, home_base, F32, after=(tok_out,))
        grad_in = run_combine(back_d1, cols[1], False, part, col, home_base, BF)
        grads = [jnp.stack([g0[i], g1[i]]) for i in range(3)]
        return tok_out, grad_in, grads[0], grads[1], jnp.swapaxes(grads[2], 1, 2)

    return jax.shard_map(moe_step, mesh=mesh, in_specs=(row_spec, row_spec, row_spec, wide_spec, wide_spec, down_spec, row_spec), out_specs=(row_spec, row_spec, wide_out, wide_out, down_out), check_vma=False)
```

time: 1400 us -> 1020 us (0.73)
  local copies, waits for them, and re-layouts: 481 us -> 19.7 us
  Pallas kernels: 0 us -> 406 us
  matrix products: 358 us -> 0 us
  other arithmetic: 149 us -> 10.4 us
  starting transfers between devices: 28 us -> 128 us
  waiting for transfers between devices: 358 us -> 434 us
    ppermute x0 -> x54, waiting for transfers between devices: none -> 434 us  [shift(): lax.ppermute(v, 'expert', [(2 * c + k, 2 * ((c + steps) % chips) + (k ^ f...]
    pallas_call x0 -> x8, Pallas kernels: none -> 406 us  [the longest x2 221 us: run_bwd(): pl.pallas_call(functools.partial(bwd_kernel, tuple((len(ts) for ts in tab...]
    dot_general x9 -> x0, matrix products: 358 us -> none  [the longest x1 81.2 us: local_step(): jnp.einsum('lscd,lfd->lscf', recv_cots, wd_full, preferred_element_type=j...]
    all_to_all x4 -> x0, waiting for transfers between devices: 356 us -> none  [the longest x1 111 us: local_step(): recv_rows = lax.all_to_all(send_rows, 'expert', 1, 1, tiled=True)]
    gather x39 -> x0, local copies, waits for them, and re-layouts: 355 us -> none  [the longest x5 232 us: gather_rows(): return jnp.take(table, index, axis=0, mode='fill', fill_value=0)]
    ppermute x0 -> x54, starting transfers between devices: none -> 128 us  [shift(): lax.ppermute(v, 'expert', [(2 * c + k, 2 * ((c + steps) % chips) + (k ^ f...]
    convert_element_type x4 -> x0, local copies, waits for them, and re-layouts: 83.6 us -> none  [the longest x1 28.6 us: local_step(): pair_grad.astype(jnp.float32)]
    reduce_sum x2 -> x0, other arithmetic: 58.5 us -> none  [the longest x1 36.9 us: local_step(): jnp.sum(pair_grad.astype(jnp.float32), axis=1)]
  transfers between devices with their start and end apart: 10 -> 58, of which waited for: 4 -> 20; matrix products, arithmetic and copies ran while one was open for 45% -> 1% of each run, Pallas kernels for 0% -> 18%
where the time goes in v1:
time: 1020 us; the launch traced here: 1010 us
  waiting for transfers between devices  434 us (43%)
  Pallas kernels  406 us (40%)
  starting transfers between devices  128 us (13%)
  local copies, waits for them, and re-layouts  19.7 us (2%)
  between operations  14.5 us (1%)
  other arithmetic  10.4 us (1%)
    ppermute x54, waiting for transfers between devices, shift(): lax.ppermute(v, 'expert', [(2 * c + k, 2 * ((c + steps) % chips) + (k ^ f...  434 us
    pallas_call x2, Pallas kernels, run_bwd(): pl.pallas_call(functools.partial(bwd_kernel, tuple((len(ts) for ts in tab...  221 us
    ppermute x54, starting transfers between devices, shift(): lax.ppermute(v, 'expert', [(2 * c + k, 2 * ((c + steps) % chips) + (k ^ f...  128 us
    pallas_call x2, Pallas kernels, run_fwd(): pl.pallas_call(functools.partial(fwd_kernel, tuple((len(ts) for ts in tab...  127 us
    pallas_call x3, Pallas kernels, run_combine(): pl.pallas_call(functools.partial(combine_kernel, tuple(cols), n, gated, l...  55.3 us
  transfers between devices with their start and end apart: 58, of which 20 were waited for; matrix products, arithmetic and copies ran while one was open for 1% of the time, Pallas kernels for 18%

profile of v1, /device:TPU:97, one launch (start us, length us, event | category | flops | bytes accessed | tf_op | source)
XLA Modules:
  0.0 1013.1 jit_solution(15459706935092246580)
XLA Ops:
  7.3 2.2 slice_bitcast_fusion
  9.5 1.1 slice_bitcast_fusion.1
  10.6 1.3 fusion.8
  12.1 2.8 fusion.10
  15.0 1.9 fusion.18
  16.9 2.2 collective-permute-start.8
  19.1 1.3 collective-permute-start.9
  20.4 1.3 collective-permute-start.12
  22.6 2.9 route.1
  26.4 1.6 collective-permute-start
  29.4 59.4 %collective-permute-done.1 = f32[2,2,2048]{2,1,0:T(2,128)S(1)} collective-permute-done((f32[2,2,2048]{2,1,0:T(2,128)S(1)}, f32[2,2,2048]{2,1,0:T(2,128)S(1)}, u32[]{:S(2)}, u32[]{:S(2)}) %collective-permute-start.1) | collective-permute-done | bytes 32800 | tf_op jit(solution)/shard_map/ppermute | solution.py:384
  88.8 1.8 collective-permute-start.3
  90.7 2.3 collective-permute-start.4
  93.0 1.4 collective-permute-start.5
  94.5 3.5 collective-permute-start.6
  98.0 2.1 fusion.17
  100.1 3.0 collective-permute-start.13
  103.2 2.6 collective-permute-start.32
  107.7 29.3 %collective-permute-done.13.refs_7_ = bf16[1024,768]{1,0:T(8,128)(2,1)} collective-permute-done((bf16[1024,768]{1,0:T(8,128)(2,1)}, bf16[1024,768]{1,0:T(8,128)(2,1)}, u32[]{:S(2)}, u32[]{:S(2)}) %collective-permute-start.13) | collective-permute-done | bytes 1572896 | tf_op jit(solution)/shard_map/ppermute | solution.py:384
  137.0 1.6 collective-permute-start.27
  138.6 1.4 collective-permute-done.28.refs_2_
  139.9 2.0 collective-permute-start.33
  142.0 31.6 %collective-permute-done.29.refs_3_ = bf16[1024,768]{1,0:T(8,128)(2,1)S(1)} collective-permute-done((bf16[1024,768]{1,0:T(8,128)(2,1)S(1)}, bf16[1024,768]{1,0:T(8,128)(2,1)S(1)}, u32[]{:S(2)}, u32[]{:S(2)}) %collective-permute-start.29) | collective-permute-done | bytes 1572896 | tf_op jit(solution)/shard_map/ppermute | solution.py:384
  173.5 1.3 collective-permute-start.10
  175.0 29.4 %collective-permute-done.33.refs_7_ = bf16[1024,768]{1,0:T(8,128)(2,1)S(1)} collective-permute-done((bf16[1024,768]{1,0:T(8,128)(2,1)S(1)}, bf16[1024,768]{1,0:T(8,128)(2,1)S(1)}, u32[]{:S(2)}, u32[]{:S(2)}) %collective-permute-start.33) | collective-permute-done | bytes 1572896 | tf_op jit(solution)/shard_map/ppermute | solution.py:384
  204.3 1.7 copy-done.1
  207.1 3.3 collective-permute-start.17
  212.0 2.2 collective-permute-done.14.refs_8_
  214.9 27.0 %collective-permute-done.16.refs_10_ = bf16[1024,768]{1,0:T(8,128)(2,1)} collective-permute-done((bf16[1024,768]{1,0:T(8,128)(2,1)}, bf16[1024,768]{1,0:T(8,128)(2,1)}, u32[]{:S(2)}, u32[]{:S(2)}) %collective-permute-start.16) | collective-permute-done | bytes 1572896 | tf_op jit(solution)/shard_map/ppermute | solution.py:384
  241.8 1.4 collective-permute-start.37
  243.2 1.3 collective-permute-done.17.refs_11_
  244.5 2.3 collective-permute-start.18
  246.9 49.1 %shard_map.110 = (bf16[2,640,768]{2,1,0:T(8,128)(2,1)}, bf16[2,640,768]{2,1,0:T(8,128)(2,1)}, bf16[2,640,768]{2,1,0:T(8,128)(2,1)}, bf16[2,640,768]{2,1,0:T(8,12...) custom-call(s32[128]{0:T(128)} %fusion.14.base_ref, ...), custom_call_target="tpu_custom_call" | custom-call | flops 24914165760 | bytes 72000000 | tf_op jit(solution)/shard_map/pallas_call | solution.py:213
  297.5 77.8 %shard_map.111 = (bf16[2,640,768]{2,1,0:T(8,128)(2,1)}, bf16[2,640,768]{2,1,0:T(8,128)(2,1)}, bf16[2,640,768]{2,1,0:T(8,128)(2,1)}, bf16[2,640,768]{2,1,0:T(8,12...) custom-call(s32[128]{0:T(128)} %fusion.14.base_ref, ...), custom_call_target="tpu_custom_call", output_to_operand_aliasing={{0}: (17, {}), {1}: (18, {}), {2}: (19, {}), {3}: (20, {}),... | custom-call | flops 41523609600 | bytes 120000000 | tf_op jit(solution)/shard_map/pallas_call | solution.py:213
  375.4 110.5 %shard_map.112 = (bf16[1,640,768]{2,1,0:T(8,128)(2,1)}, bf16[1,640,768]{2,1,0:T(8,128)(2,1)}, bf16[1,640,768]{2,1,0:T(8,128)(2,1)}, bf16[1,640,768]{2,1,0:T(8,12...) custom-call(s32[128]{0:T(128)} %fusion.14.base_ref, ...), custom_call_target="tpu_custom_call" | custom-call | flops 66437775360 | bytes 96000000 | tf_op jit(solution)/shard_map/pallas_call | solution.py:300
  485.8 110.2 %shard_map.113 = (bf16[1,640,768]{2,1,0:T(8,128)(2,1)}, bf16[1,640,768]{2,1,0:T(8,128)(2,1)}, bf16[1,640,768]{2,1,0:T(8,128)(2,1)}, bf16[1,640,768]{2,1,0:T(8,12...) custom-call(s32[128]{0:T(128)} %fusion.14.base_ref, ...), custom_call_target="tpu_custom_call" | custom-call | flops 66437775360 | bytes 96000000 | tf_op jit(solution)/shard_map/pallas_call | solution.py:300
  596.9 2.6 collective-permute-start.41
  600.8 1.5 collective-permute-start.50
  602.2 18.6 %collective-permute-done.41.refs_2_ = bf16[1,640,768]{2,1,0:T(8,128)(2,1)S(1)} collective-permute-done((bf16[1,640,768]{2,1,0:T(8,128)(2,1)}, bf16[1,640,768]{2,1,0:T(8,128)(2,1)S(1)}, u32[]{:S(2)}, u32[]{:S(2)}) %collective-permute-start.41) | collective-permute-done | bytes 983072 | tf_op jit(solution)/shard_map/ppermute | solution.py:384
  621.8 1.6 collective-permute-start.20
  624.4 3.3 collective-permute-start.21
  627.7 14.2 %collective-permute-done.48.refs_2_ = bf16[1,640,768]{2,1,0:T(8,128)(2,1)S(1)} collective-permute-done((bf16[1,640,768]{2,1,0:T(8,128)(2,1)}, bf16[1,640,768]{2,1,0:T(8,128)(2,1)S(1)}, u32[]{:S(2)}, u32[]{:S(2)}) %collective-permute-start.48) | collective-permute-done | bytes 983072 | tf_op jit(solution)/shard_map/ppermute | solution.py:384
  641.9 1.9 collective-permute-start.51
  643.8 20.3 %collective-permute-done.49.refs_3_ = bf16[1,640,768]{2,1,0:T(8,128)(2,1)S(1)} collective-permute-done((bf16[1,640,768]{2,1,0:T(8,128)(2,1)}, bf16[1,640,768]{2,1,0:T(8,128)(2,1)S(1)}, u32[]{:S(2)}, u32[]{:S(2)}) %collective-permute-start.49) | collective-permute-done | bytes 983072 | tf_op jit(solution)/shard_map/ppermute | solution.py:384
  664.1 2.5 collective-permute-start.52
  668.7 2.2 collective-permute-start.22
  670.9 19.7 %collective-permute-done.52.refs_6_ = bf16[1,640,768]{2,1,0:T(8,128)(2,1)S(1)} collective-permute-done((bf16[1,640,768]{2,1,0:T(8,128)(2,1)}, bf16[1,640,768]{2,1,0:T(8,128)(2,1)S(1)}, u32[]{:S(2)}, u32[]{:S(2)}) %collective-permute-start.52) | collective-permute-done | bytes 983072 | tf_op jit(solution)/shard_map/ppermute | solution.py:384
  690.5 37.6 %collective-permute-start.23 = (bf16[2,640,768]{2,1,0:T(8,128)(2,1)}, bf16[2,640,768]{2,1,0:T(8,128)(2,1)}, u32[]{:S(2)}, u32[]{:S(2)}) collective-permute-start(bf16[2,640,768]{2,1,0:T(8,128)(2,1)} %get-tuple-element.59), channel_id=1, source_target_pairs={{0,2},{1,3},{2,4},{3,5},{4,6},{5,7},{6,0},{7,1},{8,10},{9,11},{10,... | collective-permute-start | bytes 5898248 | tf_op jit(solution)/shard_map/ppermute | solution.py:384
  728.1 21.3 %collective-permute-start.24 = (bf16[2,640,768]{2,1,0:T(8,128)(2,1)}, bf16[2,640,768]{2,1,0:T(8,128)(2,1)}, u32[]{:S(2)}, u32[]{:S(2)}) collective-permute-start(bf16[2,640,768]{2,1,0:T(8,128)(2,1)} %get-tuple-element.60), channel_id=1, source_target_pairs={{0,3},{1,2},{2,5},{3,4},{4,7},{5,6},{6,1},{7,0},{8,11},{9,10},{10,... | collective-permute-start | bytes 5898248 | tf_op jit(solution)/shard_map/ppermute | solution.py:384
  751.7 3.4 collective-permute-start.26
  756.0 117.4 %collective-permute-done.22.refs_3_ = bf16[2,640,768]{2,1,0:T(8,128)(2,1)} collective-permute-done((bf16[2,640,768]{2,1,0:T(8,128)(2,1)}, bf16[2,640,768]{2,1,0:T(8,128)(2,1)}, u32[]{:S(2)}, u32[]{:S(2)}) %collective-permute-start.22) | collective-permute-done | bytes 1966112 | tf_op jit(solution)/shard_map/ppermute | solution.py:384
  873.5 3.8 collective-permute-start.42
  877.4 4.3 collective-permute-start.45
  881.8 19.8 %collective-permute-done.26.refs_7_ = bf16[2,640,768]{2,1,0:T(8,128)(2,1)} collective-permute-done((bf16[2,640,768]{2,1,0:T(8,128)(2,1)}, bf16[2,640,768]{2,1,0:T(8,128)(2,1)}, u32[]{:S(2)}, u32[]{:S(2)}) %collective-permute-start.26) | collective-permute-done | bytes 1966112 | tf_op jit(solution)/shard_map/ppermute | solution.py:384
  901.5 27.2 %shard_map.114.refs_8_ = bf16[2048,768]{1,0:T(8,128)(2,1)} custom-call(s32[256]{0:T(256)} %fusion.13.base_ref, bf16[2,640,768]{2,1,0:T(8,128)(2,1)} %get-tuple-element.55.refs_0_, bf16[2,640,768]{2,1,0:T(8,128)(2,1)} %copy-done.8, bf16[2,640,768]{2,1,0:T(8,128)(2,1)} %copy-done.9, bf16[2,640,768]{2,1,0:T(8,128)(2,1)} %collective-permute-done.22.refs_3_, ...), custom_call_target="tpu_custom_call" | custom-call | flops 12884901888 | bytes 20000000 | tf_op jit(solution)/shard_map/pallas_call | solution.py:357
  928.7 14.1 %shard_map.115.refs_8_ = f32[2048,768]{1,0:T(8,128)} custom-call(s32[256]{0:T(256)} %fusion.13.base_ref, bf16[1,640,768]{2,1,0:T(8,128)(2,1)} %get-tuple-element.77.refs_0_, bf16[1,640,768]{2,1,0:T(8,128)(2,1)} %copy-done.17, bf16[1,640,768]{2,1,0:T(8,128)(2,1)} %copy-done.18, bf16[1,640,768]{2,1,0:T(8,128)(2,1)} %copy-done.19, ...), custom_call_target="tpu_custom_call" | custom-call | flops 6442450944 | bytes 20000000 | tf_op jit(solution)/shard_map/pallas_call | solution.py:357
  943.7 16.1 %collective-permute-done.45.refs_6_ = bf16[1,640,768]{2,1,0:T(8,128)(2,1)} collective-permute-done((bf16[1,640,768]{2,1,0:T(8,128)(2,1)}, bf16[1,640,768]{2,1,0:T(8,128)(2,1)}, u32[]{:S(2)}, u32[]{:S(2)}) %collective-permute-start.45) | collective-permute-done | bytes 983072 | tf_op jit(solution)/shard_map/ppermute | solution.py:384
  959.8 23.4 %collective-permute-done.46.refs_7_ = bf16[1,640,768]{2,1,0:T(8,128)(2,1)} collective-permute-done((bf16[1,640,768]{2,1,0:T(8,128)(2,1)S(1)}, bf16[1,640,768]{2,1,0:T(8,128)(2,1)}, u32[]{:S(2)}, u32[]{:S(2)}) %collective-permute-start.46) | collective-permute-done | bytes 983072 | tf_op jit(solution)/shard_map/ppermute | solution.py:384
  983.2 14.1 %shard_map.116 = bf16[2048,768]{1,0:T(8,128)(2,1)} custom-call(s32[256]{0:T(256)} %fusion.13.base_ref, bf16[1,640,768]{2,1,0:T(8,128)(2,1)} %get-tuple-element.69.refs_0_, bf16[1,640,768]{2,1,0:T(8,128)(2,1)} %copy-done.15, bf16[1,640,768]{2,1,0:T(8,128)(2,1)} %copy-done.16, bf16[1,640,768]{2,1,0:T(8,128)(2,1)} %collective-permute-done.42.refs_3_, ...), custom_call_target="tpu_custom_call" | custom-call | flops 6442450944 | bytes 20000000 | tf_op jit(solution)/shard_map/pallas_call | solution.py:357
  997.3 2.1 fusion.16
  999.4 2.1 fusion.15
  1001.5 1.6 pad_maximum_fusion
  1003.1 1.6 pad_maximum_fusion.1
  1004.7 1.6 maximum_bitcast_fusion
  (147 shorter events, 21.1 us)
Async XLA Ops:
  7.2 239.7 %all-gather.3.cloned.1.call-start = ((), (), s32[]{:S(2)}) async-start(), calls=%async_computation.2 | async-start | bytes 8110080 | tf_op jit(solution)/shard_map/all_gather | solution.py:409
  12.0 285.5 %all-gather.5.cloned.1.call-start = ((), (), s32[]{:S(2)}) async-start(), calls=%async_computation.3 | async-start | bytes 8110080 | tf_op jit(solution)/shard_map/all_gather | solution.py:409
  15.0 982.3 %reduce-scatter.5.cloned.1.call-start = ((), (), s32[]{:S(2)}) async-start(), calls=%async_computation.5 | async-start | bytes 16220160 | tf_op jit(solution)/shard_map/reduce_scatter | solution.py:434
  16.9 86.2 %collective-permute-start.8 = (bf16[1024,768]{1,0:T(8,128)(2,1)}, bf16[1024,768]{1,0:T(8,128)(2,1)}, u32[]{:S(2)}, u32[]{:S(2)}) collective-permute-start(bf16[1024,768]{1,0:T(8,128)(2,1)} %get-tuple-element.94), channel_id=1, source_target_pairs={{0,2},{1,3},{2,4},{3,5},{4,6},{5,7},{6,0},{7,1},{8,10},{9,11},{10,... | collective-permute-start | bytes 4718600 | tf_op jit(solution)/shard_map/ppermute | solution.py:384
  19.1 84.1 %collective-permute-start.9 = (bf16[1024,768]{1,0:T(8,128)(2,1)}, bf16[1024,768]{1,0:T(8,128)(2,1)}, u32[]{:S(2)}, u32[]{:S(2)}) collective-permute-start(bf16[1024,768]{1,0:T(8,128)(2,1)} %get-tuple-element.93), channel_id=1, source_target_pairs={{0,2},{1,3},{2,4},{3,5},{4,6},{5,7},{6,0},{7,1},{8,10},{9,11},{10,... | collective-permute-start | bytes 4718600 | tf_op jit(solution)/shard_map/ppermute | solution.py:384
  20.4 85.4 %collective-permute-start.12 = (bf16[1024,768]{1,0:T(8,128)(2,1)}, bf16[1024,768]{1,0:T(8,128)(2,1)}, u32[]{:S(2)}, u32[]{:S(2)}) collective-permute-start(bf16[1024,768]{1,0:T(8,128)(2,1)} %get-tuple-element.94), channel_id=1, source_target_pairs={{0,6},{1,7},{2,0},{3,1},{4,2},{5,3},{6,4},{7,5},{8,14},{9,15},{10,... | collective-permute-start | bytes 4718600 | tf_op jit(solution)/shard_map/ppermute | solution.py:384
  26.4 2.4 collective-permute-start
  27.9 60.9 %collective-permute-start.1 = (f32[2,2,2048]{2,1,0:T(2,128)S(1)}, f32[2,2,2048]{2,1,0:T(2,128)S(1)}, u32[]{:S(2)}, u32[]{:S(2)}) collective-permute-start(f32[2,2,2048]{2,1,0:T(2,128)S(1)} %get-tuple-element.106), channel_id=1, source_target_pairs={{0,2},{1,3},{2,4},{3,5},{4,6},{5,7},{6,0},{7,1},{8,10},{9,11},{10,... | collective-permute-start | bytes 98312 | tf_op jit(solution)/shard_map/ppermute | solution.py:384
  28.8 61.9 %collective-permute-start.2 = (f32[2,2,2048]{2,1,0:T(2,128)S(1)}, f32[2,2,2048]{2,1,0:T(2,128)S(1)}, u32[]{:S(2)}, u32[]{:S(2)}) collective-permute-start(f32[2,2,2048]{2,1,0:T(2,128)S(1)} %get-tuple-element.105), channel_id=1, source_target_pairs={{0,3},{1,2},{2,5},{3,4},{4,7},{5,6},{6,1},{7,0},{8,11},{9,10},{10,... | collective-permute-start | bytes 98312 | tf_op jit(solution)/shard_map/ppermute | solution.py:384
  88.8 4.1 collective-permute-start.3
  90.7 3.8 collective-permute-start.4
  93.0 7.1 collective-permute-start.5
  94.5 8.6 collective-permute-start.6
  100.1 36.9 %collective-permute-start.13 = (bf16[1024,768]{1,0:T(8,128)(2,1)}, bf16[1024,768]{1,0:T(8,128)(2,1)}, u32[]{:S(2)}, u32[]{:S(2)}) collective-permute-start(bf16[1024,768]{1,0:T(8,128)(2,1)} %get-tuple-element.93), channel_id=1, source_target_pairs={{0,6},{1,7},{2,0},{3,1},{4,2},{5,3},{6,4},{7,5},{8,14},{9,15},{10,... | collective-permute-start | bytes 4718600 | tf_op jit(solution)/shard_map/ppermute | solution.py:384
  103.1 36.9 %collective-permute-start.28 = (bf16[1024,768]{1,0:T(8,128)(2,1)S(1)}, bf16[1024,768]{1,0:T(8,128)(2,1)S(1)}, u32[]{:S(2)}, u32[]{:S(2)}) collective-permute-start(bf16[1024,768]{1,0:T(8,128)(2,1)S(1)} %get-tuple-element.92), channel_id=1, source_target_pairs={{0,2},{1,3},{2,4},{3,5},{4,6},{5,7},{6,0},{7,1},{8,10},{9,11},{10,... | collective-permute-start | bytes 4718600 | tf_op jit(solution)/shard_map/ppermute | solution.py:384
  103.1 70.5 %collective-permute-start.29 = (bf16[1024,768]{1,0:T(8,128)(2,1)S(1)}, bf16[1024,768]{1,0:T(8,128)(2,1)S(1)}, u32[]{:S(2)}, u32[]{:S(2)}) collective-permute-start(bf16[1024,768]{1,0:T(8,128)(2,1)S(1)} %get-tuple-element.91), channel_id=1, source_target_pairs={{0,2},{1,3},{2,4},{3,5},{4,6},{5,7},{6,0},{7,1},{8,10},{9,11},{10,... | collective-permute-start | bytes 4718600 | tf_op jit(solution)/shard_map/ppermute | solution.py:384
  103.2 71.6 %collective-permute-start.32 = (bf16[1024,768]{1,0:T(8,128)(2,1)S(1)}, bf16[1024,768]{1,0:T(8,128)(2,1)S(1)}, u32[]{:S(2)}, u32[]{:S(2)}) collective-permute-start(bf16[1024,768]{1,0:T(8,128)(2,1)S(1)} %get-tuple-element.92), channel_id=1, source_target_pairs={{0,6},{1,7},{2,0},{3,1},{4,2},{5,3},{6,4},{7,5},{8,14},{9,15},{10,... | collective-permute-start | bytes 4718600 | tf_op jit(solution)/shard_map/ppermute | solution.py:384
  105.9 98.5 %collective-permute-start.7 = (bf16[2048,768]{1,0:T(8,128)(2,1)S(1)}, bf16[2048,768]{1,0:T(8,128)(2,1)S(1)}, u32[]{:S(2)}, u32[]{:S(2)}) collective-permute-start(bf16[2048,768]{1,0:T(8,128)(2,1)S(1)} %copy-done), channel_id=1, source_target_pairs={{0,1},{1,0},{2,3},{3,2},{4,5},{5,4},{6,7},{7,6},{8,9},{9,8},{10,11... | collective-permute-start | bytes 9437192 | tf_op jit(solution)/shard_map/ppermute | solution.py:384
  137.0 109.7 %collective-permute-start.27 = (bf16[2048,768]{1,0:T(8,128)(2,1)}, bf16[2048,768]{1,0:T(8,128)(2,1)}, u32[]{:S(2)}, u32[]{:S(2)}) collective-permute-start(bf16[2048,768]{1,0:T(8,128)(2,1)} %refs_9_.3), channel_id=1, source_target_pairs={{0,1},{1,0},{2,3},{3,2},{4,5},{5,4},{6,7},{7,6},{8,9},{9,8},{10,11... | collective-permute-start | bytes 9437192 | tf_op jit(solution)/shard_map/ppermute | solution.py:384
  139.9 64.4 %collective-permute-start.33 = (bf16[1024,768]{1,0:T(8,128)(2,1)S(1)}, bf16[1024,768]{1,0:T(8,128)(2,1)S(1)}, u32[]{:S(2)}, u32[]{:S(2)}) collective-permute-start(bf16[1024,768]{1,0:T(8,128)(2,1)S(1)} %get-tuple-element.91), channel_id=1, source_target_pairs={{0,6},{1,7},{2,0},{3,1},{4,2},{5,3},{6,4},{7,5},{8,14},{9,15},{10,... | collective-permute-start | bytes 4718600 | tf_op jit(solution)/shard_map/ppermute | solution.py:384
  173.5 33.5 %collective-permute-start.10 = (bf16[1024,768]{1,0:T(8,128)(2,1)}, bf16[1024,768]{1,0:T(8,128)(2,1)}, u32[]{:S(2)}, u32[]{:S(2)}) collective-permute-start(bf16[1024,768]{1,0:T(8,128)(2,1)} %collective-permute-done.8.refs_2_), channel_id=1, source_target_pairs={{0,1},{1,0},{2,3},{3,2},{4,5},{5,4},{6,7},{7,6},{8,9},{9,8},{10,11... | collective-permute-start | bytes 4718600 | tf_op jit(solution)/shard_map/ppermute | solution.py:384
  174.8 35.6 %collective-permute-start.11 = (bf16[1024,768]{1,0:T(8,128)(2,1)}, bf16[1024,768]{1,0:T(8,128)(2,1)}, u32[]{:S(2)}, u32[]{:S(2)}) collective-permute-start(bf16[1024,768]{1,0:T(8,128)(2,1)} %collective-permute-done.9.refs_3_), channel_id=1, source_target_pairs={{0,1},{1,0},{2,3},{3,2},{4,5},{5,4},{6,7},{7,6},{8,9},{9,8},{10,11... | collective-permute-start | bytes 4718600 | tf_op jit(solution)/shard_map/ppermute | solution.py:384
  204.3 37.5 %collective-permute-start.16 = (bf16[1024,768]{1,0:T(8,128)(2,1)}, bf16[1024,768]{1,0:T(8,128)(2,1)}, u32[]{:S(2)}, u32[]{:S(2)}) collective-permute-start(bf16[1024,768]{1,0:T(8,128)(2,1)} %collective-permute-done.8.refs_2_), channel_id=1, source_target_pairs={{0,2},{1,3},{2,4},{3,5},{4,6},{5,7},{6,0},{7,1},{8,10},{9,11},{10,... | collective-permute-start | bytes 4718600 | tf_op jit(solution)/shard_map/ppermute | solution.py:384
  206.0 8.4 collective-permute-start.15
  207.1 37.4 %collective-permute-start.17 = (bf16[1024,768]{1,0:T(8,128)(2,1)}, bf16[1024,768]{1,0:T(8,128)(2,1)}, u32[]{:S(2)}, u32[]{:S(2)}) collective-permute-start(bf16[1024,768]{1,0:T(8,128)(2,1)} %collective-permute-done.13.refs_7_), channel_id=1, source_target_pairs={{0,6},{1,7},{2,0},{3,1},{4,2},{5,3},{6,4},{7,5},{8,14},{9,15},{10,... | collective-permute-start | bytes 4718600 | tf_op jit(solution)/shard_map/ppermute | solution.py:384
  210.4 3.8 collective-permute-start.14
  214.2 81.8 %collective-permute-start.30 = (bf16[1024,768]{1,0:T(8,128)(2,1)}, bf16[1024,768]{1,0:T(8,128)(2,1)}, u32[]{:S(2)}, u32[]{:S(2)}) collective-permute-start(bf16[1024,768]{1,0:T(8,128)(2,1)} %copy-done.10), channel_id=1, source_target_pairs={{0,1},{1,0},{2,3},{3,2},{4,5},{5,4},{6,7},{7,6},{8,9},{9,8},{10,11... | collective-permute-start | bytes 4718600 | tf_op jit(solution)/shard_map/ppermute | solution.py:384
  214.5 82.0 %collective-permute-start.36 = (bf16[1024,768]{1,0:T(8,128)(2,1)}, bf16[1024,768]{1,0:T(8,128)(2,1)}, u32[]{:S(2)}, u32[]{:S(2)}) collective-permute-start(bf16[1024,768]{1,0:T(8,128)(2,1)} %copy-done.10), channel_id=1, source_target_pairs={{0,2},{1,3},{2,4},{3,5},{4,6},{5,7},{6,0},{7,1},{8,10},{9,11},{10,... | collective-permute-start | bytes 4718600 | tf_op jit(solution)/shard_map/ppermute | solution.py:384
  241.8 54.8 %collective-permute-start.37 = (bf16[1024,768]{1,0:T(8,128)(2,1)}, bf16[1024,768]{1,0:T(8,128)(2,1)}, u32[]{:S(2)}, u32[]{:S(2)}) collective-permute-start(bf16[1024,768]{1,0:T(8,128)(2,1)} %copy-done.13), channel_id=1, source_target_pairs={{0,6},{1,7},{2,0},{3,1},{4,2},{5,3},{6,4},{7,5},{8,14},{9,15},{10,... | collective-permute-start | bytes 4718600 | tf_op jit(solution)/shard_map/ppermute | solution.py:384
  244.5 52.5 %collective-permute-start.18 = (bf16[1024,768]{1,0:T(8,128)(2,1)}, bf16[1024,768]{1,0:T(8,128)(2,1)}, u32[]{:S(2)}, u32[]{:S(2)}) collective-permute-start(bf16[1024,768]{1,0:T(8,128)(2,1)} %collective-permute-done.16.refs_10_), channel_id=1, source_target_pairs={{0,1},{1,0},{2,3},{3,2},{4,5},{5,4},{6,7},{7,6},{8,9},{9,8},{10,11... | collective-permute-start | bytes 4718600 | tf_op jit(solution)/shard_map/ppermute | solution.py:384
  246.8 50.4 %collective-permute-start.19 = (bf16[1024,768]{1,0:T(8,128)(2,1)}, bf16[1024,768]{1,0:T(8,128)(2,1)}, u32[]{:S(2)}, u32[]{:S(2)}) collective-permute-start(bf16[1024,768]{1,0:T(8,128)(2,1)} %collective-permute-done.17.refs_11_), channel_id=1, source_target_pairs={{0,1},{1,0},{2,3},{3,2},{4,5},{5,4},{6,7},{7,6},{8,9},{9,8},{10,11... | collective-permute-start | bytes 4718600 | tf_op jit(solution)/shard_map/ppermute | solution.py:384
  296.0 79.4 %collective-permute-start.35 = (bf16[1024,768]{1,0:T(8,128)(2,1)}, bf16[1024,768]{1,0:T(8,128)(2,1)}, u32[]{:S(2)}, u32[]{:S(2)}) collective-permute-start(bf16[1024,768]{1,0:T(8,128)(2,1)} %copy-done.13), channel_id=1, source_target_pairs={{0,1},{1,0},{2,3},{3,2},{4,5},{5,4},{6,7},{7,6},{8,9},{9,8},{10,11... | collective-permute-start | bytes 4718600 | tf_op jit(solution)/shard_map/ppermute | solution.py:384
  296.4 78.9 %collective-permute-start.31 = (bf16[1024,768]{1,0:T(8,128)(2,1)}, bf16[1024,768]{1,0:T(8,128)(2,1)}, u32[]{:S(2)}, u32[]{:S(2)}) collective-permute-start(bf16[1024,768]{1,0:T(8,128)(2,1)} %copy-done.11), channel_id=1, source_target_pairs={{0,1},{1,0},{2,3},{3,2},{4,5},{5,4},{6,7},{7,6},{8,9},{9,8},{10,11... | collective-permute-start | bytes 4718600 | tf_op jit(solution)/shard_map/ppermute | solution.py:384
  296.6 78.7 %collective-permute-start.34 = (bf16[1024,768]{1,0:T(8,128)(2,1)}, bf16[1024,768]{1,0:T(8,128)(2,1)}, u32[]{:S(2)}, u32[]{:S(2)}) collective-permute-start(bf16[1024,768]{1,0:T(8,128)(2,1)} %copy-done.12), channel_id=1, source_target_pairs={{0,1},{1,0},{2,3},{3,2},{4,5},{5,4},{6,7},{7,6},{8,9},{9,8},{10,11... | collective-permute-start | bytes 4718600 | tf_op jit(solution)/shard_map/ppermute | solution.py:384
  297.0 78.4 %collective-permute-start.38 = (bf16[1024,768]{1,0:T(8,128)(2,1)}, bf16[1024,768]{1,0:T(8,128)(2,1)}, u32[]{:S(2)}, u32[]{:S(2)}) collective-permute-start(bf16[1024,768]{1,0:T(8,128)(2,1)} %collective-permute-done.36.refs_10_), channel_id=1, source_target_pairs={{0,1},{1,0},{2,3},{3,2},{4,5},{5,4},{6,7},{7,6},{8,9},{9,8},{10,11... | collective-permute-start | bytes 4718600 | tf_op jit(solution)/shard_map/ppermute | solution.py:384
  297.1 78.2 %collective-permute-start.39 = (bf16[1024,768]{1,0:T(8,128)(2,1)}, bf16[1024,768]{1,0:T(8,128)(2,1)}, u32[]{:S(2)}, u32[]{:S(2)}) collective-permute-start(bf16[1024,768]{1,0:T(8,128)(2,1)} %collective-permute-done.37.refs_11_), channel_id=1, source_target_pairs={{0,1},{1,0},{2,3},{3,2},{4,5},{5,4},{6,7},{7,6},{8,9},{9,8},{10,11... | collective-permute-start | bytes 4718600 | tf_op jit(solution)/shard_map/ppermute | solution.py:384
  596.1 159.0 %copy-start.7 = (f32[16,2,2048]{2,1,0:T(2,128)S(1)}, f32[16,2,2048]{2,1,0:T(2,128)}, u32[]{:S(2)}) copy-start(f32[16,2,2048]{2,1,0:T(2,128)} %get-tuple-element.45) | copy-start | bytes 786436
  596.1 305.4 %copy-start.14 = (bf16[1,640,768]{2,1,0:T(8,128)(2,1)S(1)}, bf16[1,640,768]{2,1,0:T(8,128)(2,1)}, u32[]{:S(2)}) copy-start(bf16[1,640,768]{2,1,0:T(8,128)(2,1)} %get-tuple-element.76) | copy-start | bytes 2949124
  596.1 403.2 %reduce-scatter.3.cloned.1.call-start = ((), (), s32[]{:S(2)}) async-start(), calls=%async_computation.4 | async-start | bytes 16220160 | tf_op jit(solution)/shard_map/reduce_scatter | solution.py:431
  596.8 4.0 collective-permute-start.40
  596.9 23.9 %collective-permute-start.41 = (bf16[1,640,768]{2,1,0:T(8,128)(2,1)}, bf16[1,640,768]{2,1,0:T(8,128)(2,1)S(1)}, u32[]{:S(2)}, u32[]{:S(2)}) collective-permute-start(bf16[1,640,768]{2,1,0:T(8,128)(2,1)} %get-tuple-element.71), channel_id=1, source_target_pairs={{0,6},{1,7},{2,0},{3,1},{4,2},{5,3},{6,4},{7,5},{8,14},{9,15},{10,... | collective-permute-start | bytes 2949128 | tf_op jit(solution)/shard_map/ppermute | solution.py:384
  599.5 23.9 %collective-permute-start.47 = (bf16[1,640,768]{2,1,0:T(8,128)(2,1)}, bf16[1,640,768]{2,1,0:T(8,128)(2,1)S(1)}, u32[]{:S(2)}, u32[]{:S(2)}) collective-permute-start(bf16[1,640,768]{2,1,0:T(8,128)(2,1)} %get-tuple-element.78), channel_id=1, source_target_pairs={{0,1},{1,0},{2,3},{3,2},{4,5},{5,4},{6,7},{7,6},{8,9},{9,8},{10,11... | collective-permute-start | bytes 2949128 | tf_op jit(solution)/shard_map/ppermute | solution.py:384
  600.0 41.9 %collective-permute-start.48 = (bf16[1,640,768]{2,1,0:T(8,128)(2,1)}, bf16[1,640,768]{2,1,0:T(8,128)(2,1)S(1)}, u32[]{:S(2)}, u32[]{:S(2)}) collective-permute-start(bf16[1,640,768]{2,1,0:T(8,128)(2,1)} %get-tuple-element.79), channel_id=1, source_target_pairs={{0,6},{1,7},{2,0},{3,1},{4,2},{5,3},{6,4},{7,5},{8,14},{9,15},{10,... | collective-permute-start | bytes 2949128 | tf_op jit(solution)/shard_map/ppermute | solution.py:384
  600.5 63.6 %collective-permute-start.49 = (bf16[1,640,768]{2,1,0:T(8,128)(2,1)}, bf16[1,640,768]{2,1,0:T(8,128)(2,1)S(1)}, u32[]{:S(2)}, u32[]{:S(2)}) collective-permute-start(bf16[1,640,768]{2,1,0:T(8,128)(2,1)} %get-tuple-element.80), channel_id=1, source_target_pairs={{0,7},{1,6},{2,1},{3,0},{4,3},{5,2},{6,5},{7,4},{8,15},{9,14},{10,... | collective-permute-start | bytes 2949128 | tf_op jit(solution)/shard_map/ppermute | solution.py:384
  600.8 65.8 %collective-permute-start.50 = (bf16[1,640,768]{2,1,0:T(8,128)(2,1)}, bf16[1,640,768]{2,1,0:T(8,128)(2,1)S(1)}, u32[]{:S(2)}, u32[]{:S(2)}) collective-permute-start(bf16[1,640,768]{2,1,0:T(8,128)(2,1)} %get-tuple-element.81), channel_id=1, source_target_pairs={{0,2},{1,3},{2,4},{3,5},{4,6},{5,7},{6,0},{7,1},{8,10},{9,11},{10,... | collective-permute-start | bytes 2949128 | tf_op jit(solution)/shard_map/ppermute | solution.py:384
  621.8 127.6 %collective-permute-start.20 = (bf16[2,640,768]{2,1,0:T(8,128)(2,1)S(1)}, bf16[2,640,768]{2,1,0:T(8,128)(2,1)S(1)}, u32[]{:S(2)}, u32[]{:S(2)}) collective-permute-start(bf16[2,640,768]{2,1,0:T(8,128)(2,1)S(1)} %copy-done.2), channel_id=1, source_target_pairs={{0,1},{1,0},{2,3},{3,2},{4,5},{5,4},{6,7},{7,6},{8,9},{9,8},{10,11... | collective-permute-start | bytes 5898248 | tf_op jit(solution)/shard_map/ppermute | solution.py:384
  624.4 126.1 %collective-permute-start.21 = (bf16[2,640,768]{2,1,0:T(8,128)(2,1)}, bf16[2,640,768]{2,1,0:T(8,128)(2,1)S(1)}, u32[]{:S(2)}, u32[]{:S(2)}) collective-permute-start(bf16[2,640,768]{2,1,0:T(8,128)(2,1)} %get-tuple-element.57), channel_id=1, source_target_pairs={{0,6},{1,7},{2,0},{3,1},{4,2},{5,3},{6,4},{7,5},{8,14},{9,15},{10,... | collective-permute-start | bytes 5898248 | tf_op jit(solution)/shard_map/ppermute | solution.py:384
  641.9 108.6 %copy-start.18 = (bf16[1,640,768]{2,1,0:T(8,128)(2,1)}, bf16[1,640,768]{2,1,0:T(8,128)(2,1)S(1)}, u32[]{:S(2)}) copy-start(bf16[1,640,768]{2,1,0:T(8,128)(2,1)S(1)} %collective-permute-done.48.refs_2_) | copy-start | bytes 2949124
  641.9 26.8 %collective-permute-start.51 = (bf16[1,640,768]{2,1,0:T(8,128)(2,1)}, bf16[1,640,768]{2,1,0:T(8,128)(2,1)S(1)}, u32[]{:S(2)}, u32[]{:S(2)}) collective-permute-start(bf16[1,640,768]{2,1,0:T(8,128)(2,1)} %get-tuple-element.82), channel_id=1, source_target_pairs={{0,3},{1,2},{2,5},{3,4},{4,7},{5,6},{6,1},{7,0},{8,11},{9,10},{10,... | collective-permute-start | bytes 2949128 | tf_op jit(solution)/shard_map/ppermute | solution.py:384
  664.1 86.4 %copy-start.19 = (bf16[1,640,768]{2,1,0:T(8,128)(2,1)}, bf16[1,640,768]{2,1,0:T(8,128)(2,1)S(1)}, u32[]{:S(2)}) copy-start(bf16[1,640,768]{2,1,0:T(8,128)(2,1)S(1)} %collective-permute-done.49.refs_3_) | copy-start | bytes 2949124
  664.1 26.5 %collective-permute-start.52 = (bf16[1,640,768]{2,1,0:T(8,128)(2,1)}, bf16[1,640,768]{2,1,0:T(8,128)(2,1)S(1)}, u32[]{:S(2)}, u32[]{:S(2)}) collective-permute-start(bf16[1,640,768]{2,1,0:T(8,128)(2,1)} %get-tuple-element.83), channel_id=1, source_target_pairs={{0,4},{1,5},{2,6},{3,7},{4,0},{5,1},{6,2},{7,3},{8,12},{9,13},{10,... | collective-permute-start | bytes 2949128 | tf_op jit(solution)/shard_map/ppermute | solution.py:384
  666.6 83.9 %copy-start.20 = (bf16[1,640,768]{2,1,0:T(8,128)(2,1)}, bf16[1,640,768]{2,1,0:T(8,128)(2,1)S(1)}, u32[]{:S(2)}) copy-start(bf16[1,640,768]{2,1,0:T(8,128)(2,1)S(1)} %collective-permute-done.50.refs_4_) | copy-start | bytes 2949124
  666.6 61.5 %collective-permute-start.53 = (bf16[1,640,768]{2,1,0:T(8,128)(2,1)}, bf16[1,640,768]{2,1,0:T(8,128)(2,1)S(1)}, u32[]{:S(2)}, u32[]{:S(2)}) collective-permute-start(bf16[1,640,768]{2,1,0:T(8,128)(2,1)} %get-tuple-element.84), channel_id=1, source_target_pairs={{0,5},{1,4},{2,7},{3,6},{4,1},{5,0},{6,3},{7,2},{8,13},{9,12},{10,... | collective-permute-start | bytes 2949128 | tf_op jit(solution)/shard_map/ppermute | solution.py:384
  668.7 81.8 %copy-start.21 = (bf16[1,640,768]{2,1,0:T(8,128)(2,1)}, bf16[1,640,768]{2,1,0:T(8,128)(2,1)S(1)}, u32[]{:S(2)}) copy-start(bf16[1,640,768]{2,1,0:T(8,128)(2,1)S(1)} %collective-permute-done.51.refs_5_) | copy-start | bytes 2949124
  668.7 204.8 %collective-permute-start.22 = (bf16[2,640,768]{2,1,0:T(8,128)(2,1)}, bf16[2,640,768]{2,1,0:T(8,128)(2,1)}, u32[]{:S(2)}, u32[]{:S(2)}) collective-permute-start(bf16[2,640,768]{2,1,0:T(8,128)(2,1)} %get-tuple-element.58), channel_id=1, source_target_pairs={{0,7},{1,6},{2,1},{3,0},{4,3},{5,2},{6,5},{7,4},{8,15},{9,14},{10,... | collective-permute-start | bytes 5898248 | tf_op jit(solution)/shard_map/ppermute | solution.py:384
  690.5 186.8 %collective-permute-start.23 = (bf16[2,640,768]{2,1,0:T(8,128)(2,1)}, bf16[2,640,768]{2,1,0:T(8,128)(2,1)}, u32[]{:S(2)}, u32[]{:S(2)}) collective-permute-start(bf16[2,640,768]{2,1,0:T(8,128)(2,1)} %get-tuple-element.59), channel_id=1, source_target_pairs={{0,2},{1,3},{2,4},{3,5},{4,6},{5,7},{6,0},{7,1},{8,10},{9,11},{10,... | collective-permute-start | bytes 5898248 | tf_op jit(solution)/shard_map/ppermute | solution.py:384
  728.1 149.2 %collective-permute-start.24 = (bf16[2,640,768]{2,1,0:T(8,128)(2,1)}, bf16[2,640,768]{2,1,0:T(8,128)(2,1)}, u32[]{:S(2)}, u32[]{:S(2)}) collective-permute-start(bf16[2,640,768]{2,1,0:T(8,128)(2,1)} %get-tuple-element.60), channel_id=1, source_target_pairs={{0,3},{1,2},{2,5},{3,4},{4,7},{5,6},{6,1},{7,0},{8,11},{9,10},{10,... | collective-permute-start | bytes 5898248 | tf_op jit(solution)/shard_map/ppermute | solution.py:384
  749.4 128.0 %collective-permute-start.25 = (bf16[2,640,768]{2,1,0:T(8,128)(2,1)}, bf16[2,640,768]{2,1,0:T(8,128)(2,1)}, u32[]{:S(2)}, u32[]{:S(2)}) collective-permute-start(bf16[2,640,768]{2,1,0:T(8,128)(2,1)} %get-tuple-element.61), channel_id=1, source_target_pairs={{0,4},{1,5},{2,6},{3,7},{4,0},{5,1},{6,2},{7,3},{8,12},{9,13},{10,... | collective-permute-start | bytes 5898248 | tf_op jit(solution)/shard_map/ppermute | solution.py:384
  751.7 149.8 %collective-permute-start.26 = (bf16[2,640,768]{2,1,0:T(8,128)(2,1)}, bf16[2,640,768]{2,1,0:T(8,128)(2,1)}, u32[]{:S(2)}, u32[]{:S(2)}) collective-permute-start(bf16[2,640,768]{2,1,0:T(8,128)(2,1)} %get-tuple-element.62), channel_id=1, source_target_pairs={{0,5},{1,4},{2,7},{3,6},{4,1},{5,0},{6,3},{7,2},{8,13},{9,12},{10,... | collective-permute-start | bytes 5898248 | tf_op jit(solution)/shard_map/ppermute | solution.py:384
  873.5 69.4 %collective-permute-start.42 = (bf16[1,640,768]{2,1,0:T(8,128)(2,1)}, bf16[1,640,768]{2,1,0:T(8,128)(2,1)}, u32[]{:S(2)}, u32[]{:S(2)}) collective-permute-start(bf16[1,640,768]{2,1,0:T(8,128)(2,1)} %get-tuple-element.72), channel_id=1, source_target_pairs={{0,7},{1,6},{2,1},{3,0},{4,3},{5,2},{6,5},{7,4},{8,15},{9,14},{10,... | collective-permute-start | bytes 2949128 | tf_op jit(solution)/shard_map/ppermute | solution.py:384
  877.3 65.6 %collective-permute-start.43 = (bf16[1,640,768]{2,1,0:T(8,128)(2,1)}, bf16[1,640,768]{2,1,0:T(8,128)(2,1)}, u32[]{:S(2)}, u32[]{:S(2)}) collective-permute-start(bf16[1,640,768]{2,1,0:T(8,128)(2,1)} %get-tuple-element.73), channel_id=1, source_target_pairs={{0,2},{1,3},{2,4},{3,5},{4,6},{5,7},{6,0},{7,1},{8,10},{9,11},{10,... | collective-permute-start | bytes 2949128 | tf_op jit(solution)/shard_map/ppermute | solution.py:384
  877.3 66.4 %collective-permute-start.44 = (bf16[1,640,768]{2,1,0:T(8,128)(2,1)}, bf16[1,640,768]{2,1,0:T(8,128)(2,1)}, u32[]{:S(2)}, u32[]{:S(2)}) collective-permute-start(bf16[1,640,768]{2,1,0:T(8,128)(2,1)} %get-tuple-element.74), channel_id=1, source_target_pairs={{0,3},{1,2},{2,5},{3,4},{4,7},{5,6},{6,1},{7,0},{8,11},{9,10},{10,... | collective-permute-start | bytes 2949128 | tf_op jit(solution)/shard_map/ppermute | solution.py:384
  877.4 82.3 %collective-permute-start.45 = (bf16[1,640,768]{2,1,0:T(8,128)(2,1)}, bf16[1,640,768]{2,1,0:T(8,128)(2,1)}, u32[]{:S(2)}, u32[]{:S(2)}) collective-permute-start(bf16[1,640,768]{2,1,0:T(8,128)(2,1)} %get-tuple-element.75), channel_id=1, source_target_pairs={{0,4},{1,5},{2,6},{3,7},{4,0},{5,1},{6,2},{7,3},{8,12},{9,13},{10,... | collective-permute-start | bytes 2949128 | tf_op jit(solution)/shard_map/ppermute | solution.py:384
  901.5 81.6 %collective-permute-start.46 = (bf16[1,640,768]{2,1,0:T(8,128)(2,1)S(1)}, bf16[1,640,768]{2,1,0:T(8,128)(2,1)}, u32[]{:S(2)}, u32[]{:S(2)}) collective-permute-start(bf16[1,640,768]{2,1,0:T(8,128)(2,1)S(1)} %copy-done.14), channel_id=1, source_target_pairs={{0,5},{1,4},{2,7},{3,6},{4,1},{5,0},{6,3},{7,2},{8,13},{9,12},{10,... | collective-permute-start | bytes 2949128 | tf_op jit(solution)/shard_map/ppermute | solution.py:384
  (18 other events, 360.8 us)
Sparse Core Ops, SparseCore 0:
  12.1 68.5 all-gather.2
  82.2 65.4 all-gather.4
  596.2 117.6 reduce-scatter.4
  716.2 114.8 reduce-scatter.2

commit v2 on v1

--- a/solution.py
+++ b/solution.py
@@ -15,6 +15,7 @@
 RELATION = ((0, 0), (0, 1), (1, 0), (1, 1), (-1, 0), (-1, 1), (2, 0), (2, 1))
 BLK, WIN = 256, 272
 CBLK, CWIN = 128, 144
+EARLY = (2, 4)
 
 
 def nn(lhs, rhs):
@@ -83,35 +84,36 @@
         choose(index - mid, items[mid:], act)
 
 
+def row_copies(parts, buf, sem, slot):
+    row, copies = 0, []
+    for part in parts:
+        copies.append(pltpu.make_async_copy(part, buf.at[slot, pl.ds(row, part.shape[0])], sem.at[slot]))
+        row += part.shape[0]
+    return copies
+
+
 def fetch_rows(tables, buf, sem, src, slot):
     def start(parts):
-        row = 0
-        for part in parts:
-            pltpu.make_async_copy(part, buf.at[slot, pl.ds(row, part.shape[0])], sem.at[slot]).start()
-            row += part.shape[0]
+        for copy in row_copies(parts, buf, sem, slot):
+            copy.start()
 
     choose(src, tables, start)
 
 
-def await_rows(tables, buf, sem, slot):
-    row = 0
-    for part in tables[0]:
-        pltpu.make_async_copy(part, buf.at[slot, pl.ds(row, part.shape[0])], sem.at[slot]).wait()
-        row += part.shape[0]
-
-
-def stage_rows(tables, buf, sem, source):
+def stage_rows(tables, buf, sem, source, meanwhile):
     step = pl.program_id(0)
 
     @pl.when(step == 0)
     def _():
         fetch_rows(tables, buf, sem, source(0), 0)
+        meanwhile()
 
     @pl.when(step + 1 < pl.num_programs(0))
     def _():
         fetch_rows(tables, buf, sem, source(step + 1), (step + 1) % 2)
 
-    await_rows(tables, buf, sem, step % 2)
+    for copy in row_copies(tables[0], buf, sem, step % 2):
+        copy.wait()
     return step % 2
 
 
@@ -147,7 +149,7 @@
     pltpu.make_async_copy(buf.at[slot], dests[0], sem.at[slot]).wait()
 
 
-def fwd_kernel(sizes, n_w, n_skip, item, first_src, base_ref, *refs):
+def fwd_kernel(sizes, n_w, n_skip, n_loc, item, first_src, base_ref, *refs):
     n_tab, n_out = sum(sizes), len(sizes)
     tables = split_refs(refs[:n_tab], sizes)
     w_refs = refs[n_tab:n_tab + n_w]
@@ -157,17 +159,15 @@
     r_ref, h_ref, us_ref, buf, acc, ab, w, obuf, sem, osem, wsem = rest[n_out:]
     step, last = pl.program_id(0), pl.num_programs(0) - 1
     fp = h_ref.shape[1]
-    n_loc = outs[0].shape[0]
     loc, src = item(step)
     w_at = loc if n_w > 1 else 0
     w_copies = [pltpu.make_async_copy(w_refs[i], w.at[i], wsem.at[i]) for i in range(n_w)]
 
-    @pl.when(step == 0)
-    def _():
+    def load_weights():
         for copy in w_copies:
             copy.start()
 
-    slot = stage_rows(tables, buf, sem, lambda s: item(s)[1] - first_src)
+    slot = stage_rows(tables, buf, sem, lambda s: item(s)[1] - first_src, load_weights)
     gather_seats(posg_ref, base_ref, src * n_loc + loc, buf.at[slot], acc)
     r_ref[...] = acc[...].astype(BF)
 
@@ -189,7 +189,7 @@
     us_ref[:, :fp] = b * sg * (1.0 + a * (1.0 - sg))
     us_ref[:, fp:] = silu
     obuf[slot] = nt(h_ref[...], w[w_at, :, 2 * fp:]).astype(BF)
-    put(obuf, slot, [out.at[loc] for out in outs], osem, src - first_src)
+    put(obuf, slot, [out.at[jnp.minimum(loc, out.shape[0] - 1)] for out in outs], osem, src - first_src)
 
     @pl.when(step == last)
     def _():
@@ -204,14 +204,16 @@
     any_spec = pl.BlockSpec(memory_space=ANY)
     tabs = tables[sources[0]:sources[1]]
     flat = [t for ts in tabs for t in ts]
-    skip = (*outs, *kept)
+    outs = outs or [None] * (sources[1] - sources[0])
+    old = [i for i, v in enumerate(outs) if v is not None]
+    skip = (*[outs[i] for i in old], *kept)
     seat = lambda n: pl.BlockSpec((None, None, cap, n), lambda s, b: (*item(s), 0, 0))
     n_out = sources[1] - sources[0]
     n_in = 1 + len(flat) + len(ws)
-    alias = {n_in + i: i for i in range(len(outs))} | {n_in + len(outs) + i: n_out + i for i in range(len(kept))}
+    alias = {n_in + j: i for j, i in enumerate(old)} | {n_in + len(old) + i: n_out + i for i in range(len(kept))}
     kept_shape = [jax.ShapeDtypeStruct((n_loc, n_src, cap, n), t) for n, t in ((width, BF), (fp, BF), (2 * fp, F32))]
     got = pl.pallas_call(
-        functools.partial(fwd_kernel, tuple(len(ts) for ts in tabs), len(ws), len(skip), item, sources[0]),
+        functools.partial(fwd_kernel, tuple(len(ts) for ts in tabs), len(ws), len(skip), n_loc, item, sources[0]),
         grid_spec=pltpu.PrefetchScalarGridSpec(
             num_scalar_prefetch=1, grid=(num,),
             in_specs=[any_spec] * (len(flat) + len(ws) + len(skip)) + [
@@ -220,7 +222,7 @@
             scratch_shapes=[pltpu.VMEM((2, tokens, width), BF), pltpu.VMEM((cap, width), F32), pltpu.VMEM((cap, 2 * fp), F32),
                             pltpu.VMEM((len(ws), width, wide), BF), pltpu.VMEM((2, cap, width), BF),
                             pltpu.SemaphoreType.DMA((2,)), pltpu.SemaphoreType.DMA((2,)), pltpu.SemaphoreType.DMA((len(ws),))]),
-        out_shape=[jax.ShapeDtypeStruct((n_loc, cap, width), BF)] * n_out + kept_shape,
+        out_shape=[jax.ShapeDtypeStruct((1 if k in EARLY else n_loc, cap, width), BF) for k in range(*sources)] + kept_shape,
         input_output_aliases=alias,
         compiler_params=params(),
         cost_estimate=cost(2 * num * cap * width * wide, 12_000_000 * num),
@@ -228,30 +230,38 @@
     return got[:n_out], got[n_out:]
 
 
-def bwd_kernel(sizes, n_after, ffn, loc, n_loc, base_ref, *refs):
+def bwd_kernel(sizes, n_after, loc, n_loc, base_ref, *refs):
     n_tab, n_src = sum(sizes), len(sizes)
     tables = split_refs(refs[:n_tab], sizes)
     posg_ref, w_ref, r_ref, h_ref, us_ref = refs[n_tab + n_after:n_tab + n_after + 5]
     rest = refs[n_tab + n_after + 5:]
     outs = rest[:n_src]
-    dw_ref, buf, gacc, dh, r2, c2, h2, dab2, dw, stage, obuf, sem, osem, rsem, dsem = rest[n_src:]
+    dw_ref, buf, gacc, dh, w, r2, c2, h2, dab2, dw, obuf, sem, osem, rsem, dsem = rest[n_src:]
     step = pl.program_id(0)
-    cap, fp = dh.shape
+    cap, ffn = dh.shape
+    fp = h2.shape[1]
     width = c2.shape[1]
     rows = cap // 2
-    slot = stage_rows(tables, buf, sem, lambda s: s)
+    w_copy = pltpu.make_async_copy(w_ref, w, rsem.at[2])
+
+    def meanwhile():
+        w_copy.start()
+        dw[...] = jnp.zeros_like(dw)
+        for i in range(2):
+            dab2[:, i * fp + ffn:(i + 1) * fp] = jnp.zeros((2 * cap, fp - ffn), BF)
+
+    slot = stage_rows(tables, buf, sem, lambda s: s, meanwhile)
     now = pl.multiple_of(slot * cap, cap)
     copies = [pltpu.make_async_copy(r_ref.at[loc, step], r2.at[pl.ds(now, cap)], rsem.at[0]),
               pltpu.make_async_copy(h_ref.at[loc, step], h2.at[pl.ds(now, cap)], rsem.at[1])]
     for copy in copies:
         copy.start()
-
-    @pl.when(step == 0)
-    def _():
-        dw[...] = jnp.zeros_like(dw)
-
     gather_seats(posg_ref, base_ref, step * n_loc + loc, buf.at[slot], dh.at[:, pl.ds(0, width)], gacc)
     c2[pl.ds(now, cap), :] = (gacc[...] * dh[:, :width]).astype(BF)
+
+    @pl.when(step == 0)
+    def _():
+        w_copy.wait()
 
     @pl.when(step >= 2)
     def _():
@@ -260,10 +270,10 @@
     for half in range(2):
         part = pl.ds(half * rows, rows)
         here = pl.ds(pl.multiple_of(now + half * rows, rows), rows)
-        dh[part, :] = nn(c2[here, :], w_ref[:, 2 * fp:])
-        dab2[here, :fp] = (dh[part, :] * us_ref[part, :fp]).astype(BF)
-        dab2[here, fp:] = (dh[part, :] * us_ref[part, fp:]).astype(BF)
-        obuf[slot, part, :] = nt(dab2[here, :], w_ref[:, :2 * fp]).astype(BF)
+        dh[part, :] = nn(c2[here, :], w[:, 2 * fp:2 * fp + ffn])
+        dab2[here, :ffn] = (dh[part, :] * us_ref[part, :ffn]).astype(BF)
+        dab2[here, fp:fp + ffn] = (dh[part, :] * us_ref[part, fp:fp + ffn]).astype(BF)
+        obuf[slot, part, :] = nt(dab2[here, :], w[:, :2 * fp]).astype(BF)
     put(obuf, slot, [out.at[0] for out in outs], osem, step)
     for copy in copies:
         copy.wait()
@@ -275,20 +285,20 @@
 
     @pl.when(step == n_src - 1)
     def _():
+        slots = dh.shape[0] // 128
+        moves = []
+        for i in range(3):
+            for at_row in range(0, width, 128):
+                use = pl.ds(len(moves) % slots * 128, 128)
+                if len(moves) >= slots:
+                    moves[-slots].wait()
+                dh[use, :] = dw[at_row:at_row + 128, i * fp:i * fp + ffn]
+                moves.append(pltpu.make_async_copy(dh.at[use], dw_ref.at[i, pl.ds(at_row, 128)], dsem.at[len(moves) % slots]))
+                moves[-1].start()
         await_put(obuf, 0, [outs[0].at[0]], osem)
         await_put(obuf, 1, [outs[0].at[0]], osem)
-        flush = stage.shape[1]
-        copies = []
-        for i in range(3):
-            for at_row in range(0, dw.shape[0], flush):
-                use = len(copies) % 2
-                if len(copies) >= 2:
-                    copies[-2].wait()
-                stage[use] = dw[at_row:at_row + flush, i * fp:i * fp + ffn]
-                copies.append(pltpu.make_async_copy(stage.at[use], dw_ref.at[i, pl.ds(at_row, flush)], dsem.at[use]))
-                copies[-1].start()
-        for copy in copies[-2:]:
-            copy.wait()
+        for move in moves[-slots:]:
+            move.wait()
 
 
 def run_bwd(loc, base, tables, posg, w, kept, cap, ffn, after=()):
@@ -298,19 +308,18 @@
     flat = [t for ts in tables for t in ts]
     any_spec = pl.BlockSpec(memory_space=ANY)
     got = pl.pallas_call(
-        functools.partial(bwd_kernel, tuple(len(ts) for ts in tables), len(after), ffn, loc, n_loc),
+        functools.partial(bwd_kernel, tuple(len(ts) for ts in tables), len(after), loc, n_loc),
         grid_spec=pltpu.PrefetchScalarGridSpec(
             num_scalar_prefetch=1, grid=(n_src,),
             in_specs=[any_spec] * (len(flat) + len(after)) + [
                 pl.BlockSpec((None, None, 2, tokens), lambda s, b: (s, loc, 0, 0)),
-                pl.BlockSpec((width, wide), lambda s, b: (0, 0), pipeline_mode=pl.Buffered(1)),
-                any_spec, any_spec,
+                any_spec, any_spec, any_spec,
                 pl.BlockSpec((None, None, cap, 2 * fp), lambda s, b: (loc, s, 0, 0))],
             out_specs=[any_spec] * (n_src + 1),
-            scratch_shapes=[pltpu.VMEM((2, tokens, width), BF), pltpu.VMEM((cap, 1), F32), pltpu.VMEM((cap, fp), F32),
+            scratch_shapes=[pltpu.VMEM((2, tokens, width), BF), pltpu.VMEM((cap, 1), F32), pltpu.VMEM((cap, ffn), F32), pltpu.VMEM((width, wide), BF),
                             pltpu.VMEM((2 * cap, width), BF), pltpu.VMEM((2 * cap, width), BF), pltpu.VMEM((2 * cap, fp), BF), pltpu.VMEM((2 * cap, 2 * fp), BF),
-                            pltpu.VMEM((width, wide), F32), pltpu.VMEM((2, width // 6, ffn), F32), pltpu.VMEM((2, cap, width), BF),
-                            pltpu.SemaphoreType.DMA((2,)), pltpu.SemaphoreType.DMA((2,)), pltpu.SemaphoreType.DMA((2,)), pltpu.SemaphoreType.DMA((2,))]),
+                            pltpu.VMEM((width, wide), F32), pltpu.VMEM((2, cap, width), BF),
+                            pltpu.SemaphoreType.DMA((2,)), pltpu.SemaphoreType.DMA((2,)), pltpu.SemaphoreType.DMA((3,)), pltpu.SemaphoreType.DMA((cap // 128,))]),
         out_shape=[jax.ShapeDtypeStruct((1, cap, width), BF)] * n_src + [jax.ShapeDtypeStruct((3, width, ffn), F32)],
         compiler_params=pltpu.CompilerParams(vmem_limit_bytes=67_043_328, dimension_semantics=("arbitrary",)),
         cost_estimate=cost(4 * n_src * cap * width * wide, 12_000_000 * n_src),
@@ -322,11 +331,11 @@
     n = n_back
     back = refs[:n]
     start_ref, col_ref, out_ref, buf, sem = refs[n + n_after:]
-    per_back, _, _ = back[0].shape
+    starts = [sum(v.shape[0] for v in back[:i]) for i in range(n)]
     step = pl.program_id(0)
     blocks = pl.num_programs(0) * per
     n_exp = col_ref.shape[1] // 2
-    copies = [pltpu.make_async_copy(back[i], buf.at[pl.ds(i * per_back, per_back)], sem.at[i]) for i in range(n)]
+    copies = [pltpu.make_async_copy(back[i], buf.at[pl.ds(starts[i], back[i].shape[0])], sem.at[i]) for i in range(n)]
 
     @pl.when(step == 0)
     def _():
@@ -371,6 +380,32 @@
     return (jnp.minimum(first.astype(jnp.int32), cap - window) // align * align).reshape(-1)
 
 
+def place_kernel(row, n_skip, g_ref, *refs):
+    outs, (buf, sem_in, sem_out) = refs[n_skip:-3], refs[-3:]
+    ins = [pltpu.make_async_copy(g_ref.at[i], buf.at[i], sem_in.at[i]) for i in range(len(outs))]
+    puts = [pltpu.make_async_copy(buf.at[i], out.at[row], sem_out.at[i]) for i, out in enumerate(outs)]
+    for copy in ins:
+        copy.start()
+    for copy, put_out in zip(ins, puts):
+        copy.wait()
+        put_out.start()
+    for copy in puts:
+        copy.wait()
+
+
+def place(row, n_loc, g, into=()):
+    n, rows, ffn = g.shape
+    any_spec = pl.BlockSpec(memory_space=ANY)
+    return pl.pallas_call(
+        functools.partial(place_kernel, row, len(into)),
+        in_specs=[any_spec] * (1 + len(into)), out_specs=[any_spec] * n,
+        out_shape=[jax.ShapeDtypeStruct((n_loc, rows, ffn), F32)] * n,
+        scratch_shapes=[pltpu.VMEM((n, rows, ffn), F32), pltpu.SemaphoreType.DMA((n,)), pltpu.SemaphoreType.DMA((n,))],
+        input_output_aliases={1 + i: i for i in range(len(into))},
+        cost_estimate=cost(1_000_000, 2 * n * rows * ffn * 4),
+    )(g, *into)
+
+
 def solution(mesh):
     ep_size = mesh.shape["expert"]
     chips = ep_size // 2
@@ -418,11 +453,13 @@
         posg_in = jnp.stack(moved)
         base = block_base(posg_in[:, :, 0], BLK, WIN, cap, 8)
 
-        def give_back(rows):
-            return [rows[k] if k == 0 else shift(rows[k], -s, f) for k, (s, f) in enumerate(RELATION)]
+        def give_back(rows, which=range(n_src)):
+            return [v if k == 0 else shift(v, -RELATION[k][0], RELATION[k][1]) for k, v in zip(which, rows)]
 
         cut = n_src - 2
         outs, kept = run_fwd(cut, lambda s: (0, s), (0, cut), base, x_tabs, posg_in, weights[:1], cap)
+        ahead = give_back([outs[k] for k in EARLY], EARLY)
+        outs = [None if k in EARLY or k >= cut else outs[k] for k in range(n_src)]
         later = lambda s: (jnp.where(s < 2, 0, 1), jnp.where(s < 2, s + cut, s - 2))
         outs, kept = run_fwd(n_src + 2, later, (0, n_src), base, x_tabs, posg_in, weights, cap, outs, kept)
         back_o = give_back(outs)
@@ -434,10 +471,12 @@
         g1 = lax.psum_scatter(dw1, "data", scatter_dimension=1, tiled=True)
 
         cols = [[k * n_loc + e for k in range(n_src)] for e in range(n_loc)]
-        tok_out = run_combine(back_o, list(range(n_loc * n_src)), True, tok_in, col, home_base, BF, after=(dw1,))
-        part = run_combine(back_d0, cols[0], False, grad_out, col, home_base, F32, after=(tok_out,))
+        seats = [k * n_loc + e for k in range(n_src) for e in range(1 if k in EARLY else 0, n_loc)] + [k * n_loc for k in EARLY]
+        tok_out = run_combine(back_o + ahead, seats, True, tok_in, col, home_base, BF, after=(dw1,))
+        early = place(0, n_loc, g0)
+        part = run_combine(back_d0, cols[0], False, grad_out, col, home_base, F32, after=(tok_out, early[0]))
         grad_in = run_combine(back_d1, cols[1], False, part, col, home_base, BF)
-        grads = [jnp.stack([g0[i], g1[i]]) for i in range(3)]
+        grads = place(1, n_loc, g1, early)
         return tok_out, grad_in, grads[0], grads[1], jnp.swapaxes(grads[2], 1, 2)
 
     return jax.shard_map(moe_step, mesh=mesh, in_specs=(row_spec, row_spec, row_spec, wide_spec, wide_spec, down_spec, row_spec), out_specs=(row_spec, row_spec, wide_out, wide_out, down_out), check_vma=False)

time: 1020 us -> 982 us (0.963)
  waiting for transfers between devices: 434 us -> 422 us
    pallas_call x2, Pallas kernels: 221 us -> 209 us  [run_bwd(): pl.pallas_call(functools.partial(bwd_kernel, tuple((len(ts) for ts in tab...]
    ppermute x54 -> x56, waiting for transfers between devices: 434 us -> 422 us  [shift(): lax.ppermute(v, 'expert', [(2 * c + k, 2 * ((c + steps) % chips) + (k ^ f...]
    ppermute x54 -> x56, starting transfers between devices: 128 us -> 122 us  [shift(): lax.ppermute(v, 'expert', [(2 * c + k, 2 * ((c + steps) % chips) + (k ^ f...]
  transfers between devices with their start and end apart: 58 -> 60, of which waited for: 20 -> 20; matrix products, arithmetic and copies ran while one was open for 1% -> 1% of each run, Pallas kernels for 18% -> 29%
where the time goes in v2:
time: 982 us; the launch traced here: 975 us
  waiting for transfers between devices  422 us (43%)
  Pallas kernels  398 us (41%)
  starting transfers between devices  122 us (12%)
  between operations  14.5 us (1%)
  local copies, waits for them, and re-layouts  13.3 us (1%)
    ppermute x56, waiting for transfers between devices, shift(): lax.ppermute(v, 'expert', [(2 * c + k, 2 * ((c + steps) % chips) + (k ^ f...  422 us
    pallas_call x2, Pallas kernels, run_bwd(): pl.pallas_call(functools.partial(bwd_kernel, tuple((len(ts) for ts in tab...  209 us
    pallas_call x2, Pallas kernels, run_fwd(): pl.pallas_call(functools.partial(fwd_kernel, tuple((len(ts) for ts in tab...  126 us
    ppermute x56, starting transfers between devices, shift(): lax.ppermute(v, 'expert', [(2 * c + k, 2 * ((c + steps) % chips) + (k ^ f...  122 us
    pallas_call x3, Pallas kernels, run_combine(): pl.pallas_call(functools.partial(combine_kernel, tuple(cols), n, gated, l...  55.2 us
  transfers between devices with their start and end apart: 60, of which 20 were waited for; matrix products, arithmetic and copies ran while one was open for 1% of the time, Pallas kernels for 29%

profile of v2, /device:TPU:97, one launch (start us, length us, event | category | flops | bytes accessed | tf_op | source)
XLA Modules:
  0.0 975.5 jit_solution(1736457591316834623)
XLA Ops:
  7.3 2.2 slice_bitcast_fusion
  12.1 2.9 fusion.10
  15.1 1.9 fusion.16
  16.9 2.2 collective-permute-start.8
  19.1 1.3 collective-permute-start.9
  20.4 1.3 collective-permute-start.12
  22.6 2.9 route.1
  26.4 1.6 collective-permute-start
  29.4 59.4 %collective-permute-done.1 = f32[2,2,2048]{2,1,0:T(2,128)S(1)} collective-permute-done((f32[2,2,2048]{2,1,0:T(2,128)S(1)}, f32[2,2,2048]{2,1,0:T(2,128)S(1)}, u32[]{:S(2)}, u32[]{:S(2)}) %collective-permute-start.1) | collective-permute-done | bytes 32800 | tf_op jit(solution)/shard_map/ppermute | solution.py:419
  88.9 1.8 collective-permute-start.3
  90.7 2.3 collective-permute-start.4
  93.0 1.4 collective-permute-start.5
  94.5 3.5 collective-permute-start.6
  98.0 2.1 fusion.15
  100.1 3.0 collective-permute-start.13
  103.2 2.6 collective-permute-start.34
  107.8 29.3 %collective-permute-done.13.refs_7_ = bf16[1024,768]{1,0:T(8,128)(2,1)} collective-permute-done((bf16[1024,768]{1,0:T(8,128)(2,1)}, bf16[1024,768]{1,0:T(8,128)(2,1)}, u32[]{:S(2)}, u32[]{:S(2)}) %collective-permute-start.13) | collective-permute-done | bytes 1572896 | tf_op jit(solution)/shard_map/ppermute | solution.py:419
  137.0 1.6 collective-permute-start.29
  138.6 1.4 collective-permute-done.30.refs_2_
  140.0 2.0 collective-permute-start.35
  142.0 31.6 %collective-permute-done.31.refs_3_ = bf16[1024,768]{1,0:T(8,128)(2,1)S(1)} collective-permute-done((bf16[1024,768]{1,0:T(8,128)(2,1)S(1)}, bf16[1024,768]{1,0:T(8,128)(2,1)S(1)}, u32[]{:S(2)}, u32[]{:S(2)}) %collective-permute-start.31) | collective-permute-done | bytes 1572896 | tf_op jit(solution)/shard_map/ppermute | solution.py:419
  175.0 29.4 %collective-permute-done.35.refs_7_ = bf16[1024,768]{1,0:T(8,128)(2,1)S(1)} collective-permute-done((bf16[1024,768]{1,0:T(8,128)(2,1)S(1)}, bf16[1024,768]{1,0:T(8,128)(2,1)S(1)}, u32[]{:S(2)}, u32[]{:S(2)}) %collective-permute-start.35) | collective-permute-done | bytes 1572896 | tf_op jit(solution)/shard_map/ppermute | solution.py:419
  204.4 1.7 copy-done.1
  207.1 3.3 collective-permute-start.17
  212.0 2.2 collective-permute-done.14.refs_8_
  214.9 27.0 %collective-permute-done.16.refs_10_ = bf16[1024,768]{1,0:T(8,128)(2,1)} collective-permute-done((bf16[1024,768]{1,0:T(8,128)(2,1)}, bf16[1024,768]{1,0:T(8,128)(2,1)}, u32[]{:S(2)}, u32[]{:S(2)}) %collective-permute-start.16) | collective-permute-done | bytes 1572896 | tf_op jit(solution)/shard_map/ppermute | solution.py:419
  241.9 1.4 collective-permute-start.39
  243.2 1.3 collective-permute-done.17.refs_11_
  244.5 2.3 collective-permute-start.18
  246.9 49.2 %shard_map.110 = (bf16[2,640,768]{2,1,0:T(8,128)(2,1)}, bf16[2,640,768]{2,1,0:T(8,128)(2,1)}, bf16[1,640,768]{2,1,0:T(8,128)(2,1)}, bf16[2,640,768]{2,1,0:T(8,12...) custom-call(s32[128]{0:T(128)} %fusion.14.base_ref, ...), custom_call_target="tpu_custom_call" | custom-call | flops 24914165760 | bytes 72000000 | tf_op jit(solution)/shard_map/pallas_call | solution.py:215
  297.5 76.4 %shard_map.111 = (bf16[2,640,768]{2,1,0:T(8,128)(2,1)}, bf16[2,640,768]{2,1,0:T(8,128)(2,1)}, bf16[1,640,768]{2,1,0:T(8,128)(2,1)}, bf16[2,640,768]{2,1,0:T(8,12...) custom-call(s32[128]{0:T(128)} %fusion.14.base_ref, ...), custom_call_target="tpu_custom_call", output_to_operand_aliasing={{0}: (17, {}), {1}: (18, {}), {3}: (19, {}), {5}: (20, {}),... | custom-call | flops 41523609600 | bytes 120000000 | tf_op jit(solution)/shard_map/pallas_call | solution.py:215
  374.0 105.2 %shard_map.112 = (bf16[1,640,768]{2,1,0:T(8,128)(2,1)}, bf16[1,640,768]{2,1,0:T(8,128)(2,1)}, bf16[1,640,768]{2,1,0:T(8,128)(2,1)}, bf16[1,640,768]{2,1,0:T(8,12...) custom-call(s32[128]{0:T(128)} %fusion.14.base_ref, ...), custom_call_target="tpu_custom_call" | custom-call | flops 66437775360 | bytes 96000000 | tf_op jit(solution)/shard_map/pallas_call | solution.py:310
  479.3 103.4 %shard_map.113 = (bf16[1,640,768]{2,1,0:T(8,128)(2,1)}, bf16[1,640,768]{2,1,0:T(8,128)(2,1)}, bf16[1,640,768]{2,1,0:T(8,128)(2,1)}, bf16[1,640,768]{2,1,0:T(8,12...) custom-call(s32[128]{0:T(128)} %fusion.14.base_ref, ...), custom_call_target="tpu_custom_call" | custom-call | flops 66437775360 | bytes 96000000 | tf_op jit(solution)/shard_map/pallas_call | solution.py:310
  582.8 2.5 collective-permute-start.21
  585.2 2.7 collective-permute-start.27
  589.1 17.3 %collective-permute-done.21.refs_2_ = bf16[1,640,768]{2,1,0:T(8,128)(2,1)S(1)} collective-permute-done((bf16[1,640,768]{2,1,0:T(8,128)(2,1)}, bf16[1,640,768]{2,1,0:T(8,128)(2,1)S(1)}, u32[]{:S(2)}, u32[]{:S(2)}) %collective-permute-start.21) | collective-permute-done | bytes 983072 | tf_op jit(solution)/shard_map/ppermute | solution.py:419
  607.3 3.3 collective-permute-start.43
  610.6 2.2 collective-permute-start.49
  612.8 14.7 %collective-permute-done.27.refs_8_ = bf16[1,640,768]{2,1,0:T(8,128)(2,1)S(1)} collective-permute-done((bf16[1,640,768]{2,1,0:T(8,128)(2,1)}, bf16[1,640,768]{2,1,0:T(8,128)(2,1)S(1)}, u32[]{:S(2)}, u32[]{:S(2)}) %collective-permute-start.27) | collective-permute-done | bytes 983072 | tf_op jit(solution)/shard_map/ppermute | solution.py:419
  627.5 3.3 collective-permute-start.50
  630.8 1.8 collective-permute-start.51
  632.7 1.6 collective-permute-start.52
  634.3 14.3 %collective-permute-done.43.refs_2_ = bf16[1,640,768]{2,1,0:T(8,128)(2,1)S(1)} collective-permute-done((bf16[1,640,768]{2,1,0:T(8,128)(2,1)}, bf16[1,640,768]{2,1,0:T(8,128)(2,1)S(1)}, u32[]{:S(2)}, u32[]{:S(2)}) %collective-permute-start.43) | collective-permute-done | bytes 983072 | tf_op jit(solution)/shard_map/ppermute | solution.py:419
  648.6 2.0 collective-permute-start.53
  650.6 4.2 collective-permute-start.54
  654.8 14.8 %collective-permute-done.50.refs_2_ = bf16[1,640,768]{2,1,0:T(8,128)(2,1)S(1)} collective-permute-done((bf16[1,640,768]{2,1,0:T(8,128)(2,1)}, bf16[1,640,768]{2,1,0:T(8,128)(2,1)S(1)}, u32[]{:S(2)}, u32[]{:S(2)}) %collective-permute-start.50) | collective-permute-done | bytes 983072 | tf_op jit(solution)/shard_map/ppermute | solution.py:419
  669.6 4.1 collective-permute-start.55
  673.7 18.0 %collective-permute-done.51.refs_3_ = bf16[1,640,768]{2,1,0:T(8,128)(2,1)S(1)} collective-permute-done((bf16[1,640,768]{2,1,0:T(8,128)(2,1)}, bf16[1,640,768]{2,1,0:T(8,128)(2,1)S(1)}, u32[]{:S(2)}, u32[]{:S(2)}) %collective-permute-start.51) | collective-permute-done | bytes 983072 | tf_op jit(solution)/shard_map/ppermute | solution.py:419
  691.7 42.2 %collective-permute-start.20 = (bf16[2,640,768]{2,1,0:T(8,128)(2,1)S(1)}, bf16[2,640,768]{2,1,0:T(8,128)(2,1)}, u32[]{:S(2)}, u32[]{:S(2)}) collective-permute-start(bf16[2,640,768]{2,1,0:T(8,128)(2,1)S(1)} %copy-done.2), channel_id=1, source_target_pairs={{0,1},{1,0},{2,3},{3,2},{4,5},{5,4},{6,7},{7,6},{8,9},{9,8},{10,11... | collective-permute-start | bytes 5898248 | tf_op jit(solution)/shard_map/ppermute | solution.py:419
  734.0 3.0 collective-permute-start.22
  738.3 2.2 collective-permute-start.26
  741.4 2.6 collective-permute-start.44
  744.0 119.7 %collective-permute-done.22.refs_3_ = bf16[2,640,768]{2,1,0:T(8,128)(2,1)} collective-permute-done((bf16[2,640,768]{2,1,0:T(8,128)(2,1)}, bf16[2,640,768]{2,1,0:T(8,128)(2,1)}, u32[]{:S(2)}, u32[]{:S(2)}) %collective-permute-start.22) | collective-permute-done | bytes 1966112 | tf_op jit(solution)/shard_map/ppermute | solution.py:419
  863.7 3.5 collective-permute-done.24.refs_5_
  867.3 1.9 collective-permute-start.47
  869.2 1.4 collective-permute-start.48
  870.5 27.1 %shard_map.114.refs_8_ = bf16[2048,768]{1,0:T(8,128)(2,1)} custom-call(s32[256]{0:T(256)} %fusion.13.base_ref, bf16[2,640,768]{2,1,0:T(8,128)(2,1)} %get-tuple-element.59.refs_0_, bf16[2,640,768]{2,1,0:T(8,128)(2,1)} %collective-permute-done.20.refs_1_, bf16[1,640,768]{2,1,0:T(8,128)(2,1)} %copy-done.15, ...), custom_call_target="tpu_custom_call" | custom-call | flops 12884901888 | bytes 20000000 | tf_op jit(solution)/shard_map/pallas_call | solution.py:366
  897.7 3.0 shard_map.115
  900.7 14.1 %shard_map.116.refs_8_ = f32[2048,768]{1,0:T(8,128)} custom-call(s32[256]{0:T(256)} %fusion.13.base_ref, bf16[1,640,768]{2,1,0:T(8,128)(2,1)} %get-tuple-element.83.refs_0_, bf16[1,640,768]{2,1,0:T(8,128)(2,1)} %copy-done.19, bf16[1,640,768]{2,1,0:T(8,128)(2,1)} %copy-done.20, bf16[1,640,768]{2,1,0:T(8,128)(2,1)} %copy-done.21, ...), custom_call_target="tpu_custom_call" | custom-call | flops 6442450944 | bytes 20000000 | tf_op jit(solution)/shard_map/pallas_call | solution.py:366
  914.8 3.0 shard_map.118
  917.8 9.2 collective-permute-done.44.refs_3_
  926.9 6.6 collective-permute-done.47.refs_6_
  933.5 21.1 %collective-permute-done.48.refs_7_ = bf16[1,640,768]{2,1,0:T(8,128)(2,1)} collective-permute-done((bf16[1,640,768]{2,1,0:T(8,128)(2,1)S(1)}, bf16[1,640,768]{2,1,0:T(8,128)(2,1)}, u32[]{:S(2)}, u32[]{:S(2)}) %collective-permute-start.48) | collective-permute-done | bytes 983072 | tf_op jit(solution)/shard_map/ppermute | solution.py:419
  954.6 14.1 %shard_map.117 = bf16[2048,768]{1,0:T(8,128)(2,1)} custom-call(s32[256]{0:T(256)} %fusion.13.base_ref, bf16[1,640,768]{2,1,0:T(8,128)(2,1)} %get-tuple-element.75.refs_0_, bf16[1,640,768]{2,1,0:T(8,128)(2,1)} %copy-done.13, bf16[1,640,768]{2,1,0:T(8,128)(2,1)} %copy-done.14, bf16[1,640,768]{2,1,0:T(8,128)(2,1)} %collective-permute-done.44.refs_3_, ...), custom_call_target="tpu_custom_call" | custom-call | flops 6442450944 | bytes 20000000 | tf_op jit(solution)/shard_map/pallas_call | solution.py:366
  (152 shorter events, 19.0 us)
Async XLA Ops:
  7.2 239.7 %all-gather.3.cloned.1.call-start = ((), (), s32[]{:S(2)}) async-start(), calls=%async_computation.2 | async-start | bytes 8110080 | tf_op jit(solution)/shard_map/all_gather | solution.py:444
  12.0 285.6 %all-gather.5.cloned.1.call-start = ((), (), s32[]{:S(2)}) async-start(), calls=%async_computation.3 | async-start | bytes 8110080 | tf_op jit(solution)/shard_map/all_gather | solution.py:444
  15.0 882.7 %reduce-scatter.3.cloned.1.call-start = ((), (), s32[]{:S(2)}) async-start(), calls=%async_computation.4 | async-start | bytes 16220160 | tf_op jit(solution)/shard_map/reduce_scatter | solution.py:468
  16.9 86.2 %collective-permute-start.8 = (bf16[1024,768]{1,0:T(8,128)(2,1)}, bf16[1024,768]{1,0:T(8,128)(2,1)}, u32[]{:S(2)}, u32[]{:S(2)}) collective-permute-start(bf16[1024,768]{1,0:T(8,128)(2,1)} %get-tuple-element.100), channel_id=1, source_target_pairs={{0,2},{1,3},{2,4},{3,5},{4,6},{5,7},{6,0},{7,1},{8,10},{9,11},{10,... | collective-permute-start | bytes 4718600 | tf_op jit(solution)/shard_map/ppermute | solution.py:419
  19.1 84.1 %collective-permute-start.9 = (bf16[1024,768]{1,0:T(8,128)(2,1)}, bf16[1024,768]{1,0:T(8,128)(2,1)}, u32[]{:S(2)}, u32[]{:S(2)}) collective-permute-start(bf16[1024,768]{1,0:T(8,128)(2,1)} %get-tuple-element.99), channel_id=1, source_target_pairs={{0,2},{1,3},{2,4},{3,5},{4,6},{5,7},{6,0},{7,1},{8,10},{9,11},{10,... | collective-permute-start | bytes 4718600 | tf_op jit(solution)/shard_map/ppermute | solution.py:419
  20.4 85.4 %collective-permute-start.12 = (bf16[1024,768]{1,0:T(8,128)(2,1)}, bf16[1024,768]{1,0:T(8,128)(2,1)}, u32[]{:S(2)}, u32[]{:S(2)}) collective-permute-start(bf16[1024,768]{1,0:T(8,128)(2,1)} %get-tuple-element.100), channel_id=1, source_target_pairs={{0,6},{1,7},{2,0},{3,1},{4,2},{5,3},{6,4},{7,5},{8,14},{9,15},{10,... | collective-permute-start | bytes 4718600 | tf_op jit(solution)/shard_map/ppermute | solution.py:419
  26.4 2.4 collective-permute-start
  28.0 60.9 %collective-permute-start.1 = (f32[2,2,2048]{2,1,0:T(2,128)S(1)}, f32[2,2,2048]{2,1,0:T(2,128)S(1)}, u32[]{:S(2)}, u32[]{:S(2)}) collective-permute-start(f32[2,2,2048]{2,1,0:T(2,128)S(1)} %get-tuple-element.112), channel_id=1, source_target_pairs={{0,2},{1,3},{2,4},{3,5},{4,6},{5,7},{6,0},{7,1},{8,10},{9,11},{10,... | collective-permute-start | bytes 98312 | tf_op jit(solution)/shard_map/ppermute | solution.py:419
  28.8 61.9 %collective-permute-start.2 = (f32[2,2,2048]{2,1,0:T(2,128)S(1)}, f32[2,2,2048]{2,1,0:T(2,128)S(1)}, u32[]{:S(2)}, u32[]{:S(2)}) collective-permute-start(f32[2,2,2048]{2,1,0:T(2,128)S(1)} %get-tuple-element.111), channel_id=1, source_target_pairs={{0,3},{1,2},{2,5},{3,4},{4,7},{5,6},{6,1},{7,0},{8,11},{9,10},{10,... | collective-permute-start | bytes 98312 | tf_op jit(solution)/shard_map/ppermute | solution.py:419
  88.9 4.1 collective-permute-start.3
  90.7 3.8 collective-permute-start.4
  93.0 7.1 collective-permute-start.5
  94.5 8.6 collective-permute-start.6
  100.1 36.9 %collective-permute-start.13 = (bf16[1024,768]{1,0:T(8,128)(2,1)}, bf16[1024,768]{1,0:T(8,128)(2,1)}, u32[]{:S(2)}, u32[]{:S(2)}) collective-permute-start(bf16[1024,768]{1,0:T(8,128)(2,1)} %get-tuple-element.99), channel_id=1, source_target_pairs={{0,6},{1,7},{2,0},{3,1},{4,2},{5,3},{6,4},{7,5},{8,14},{9,15},{10,... | collective-permute-start | bytes 4718600 | tf_op jit(solution)/shard_map/ppermute | solution.py:419
  103.1 36.9 %collective-permute-start.30 = (bf16[1024,768]{1,0:T(8,128)(2,1)S(1)}, bf16[1024,768]{1,0:T(8,128)(2,1)S(1)}, u32[]{:S(2)}, u32[]{:S(2)}) collective-permute-start(bf16[1024,768]{1,0:T(8,128)(2,1)S(1)} %get-tuple-element.98), channel_id=1, source_target_pairs={{0,2},{1,3},{2,4},{3,5},{4,6},{5,7},{6,0},{7,1},{8,10},{9,11},{10,... | collective-permute-start | bytes 4718600 | tf_op jit(solution)/shard_map/ppermute | solution.py:419
  103.1 70.5 %collective-permute-start.31 = (bf16[1024,768]{1,0:T(8,128)(2,1)S(1)}, bf16[1024,768]{1,0:T(8,128)(2,1)S(1)}, u32[]{:S(2)}, u32[]{:S(2)}) collective-permute-start(bf16[1024,768]{1,0:T(8,128)(2,1)S(1)} %get-tuple-element.97), channel_id=1, source_target_pairs={{0,2},{1,3},{2,4},{3,5},{4,6},{5,7},{6,0},{7,1},{8,10},{9,11},{10,... | collective-permute-start | bytes 4718600 | tf_op jit(solution)/shard_map/ppermute | solution.py:419
  103.2 71.6 %collective-permute-start.34 = (bf16[1024,768]{1,0:T(8,128)(2,1)S(1)}, bf16[1024,768]{1,0:T(8,128)(2,1)S(1)}, u32[]{:S(2)}, u32[]{:S(2)}) collective-permute-start(bf16[1024,768]{1,0:T(8,128)(2,1)S(1)} %get-tuple-element.98), channel_id=1, source_target_pairs={{0,6},{1,7},{2,0},{3,1},{4,2},{5,3},{6,4},{7,5},{8,14},{9,15},{10,... | collective-permute-start | bytes 4718600 | tf_op jit(solution)/shard_map/ppermute | solution.py:419
  105.9 98.5 %collective-permute-start.7 = (bf16[2048,768]{1,0:T(8,128)(2,1)S(1)}, bf16[2048,768]{1,0:T(8,128)(2,1)S(1)}, u32[]{:S(2)}, u32[]{:S(2)}) collective-permute-start(bf16[2048,768]{1,0:T(8,128)(2,1)S(1)} %copy-done), channel_id=1, source_target_pairs={{0,1},{1,0},{2,3},{3,2},{4,5},{5,4},{6,7},{7,6},{8,9},{9,8},{10,11... | collective-permute-start | bytes 9437192 | tf_op jit(solution)/shard_map/ppermute | solution.py:419
  137.0 109.7 %collective-permute-start.29 = (bf16[2048,768]{1,0:T(8,128)(2,1)}, bf16[2048,768]{1,0:T(8,128)(2,1)}, u32[]{:S(2)}, u32[]{:S(2)}) collective-permute-start(bf16[2048,768]{1,0:T(8,128)(2,1)} %refs_10_.1), channel_id=1, source_target_pairs={{0,1},{1,0},{2,3},{3,2},{4,5},{5,4},{6,7},{7,6},{8,9},{9,8},{10,11... | collective-permute-start | bytes 9437192 | tf_op jit(solution)/shard_map/ppermute | solution.py:419
  140.0 64.4 %collective-permute-start.35 = (bf16[1024,768]{1,0:T(8,128)(2,1)S(1)}, bf16[1024,768]{1,0:T(8,128)(2,1)S(1)}, u32[]{:S(2)}, u32[]{:S(2)}) collective-permute-start(bf16[1024,768]{1,0:T(8,128)(2,1)S(1)} %get-tuple-element.97), channel_id=1, source_target_pairs={{0,6},{1,7},{2,0},{3,1},{4,2},{5,3},{6,4},{7,5},{8,14},{9,15},{10,... | collective-permute-start | bytes 4718600 | tf_op jit(solution)/shard_map/ppermute | solution.py:419
  173.6 33.5 %collective-permute-start.10 = (bf16[1024,768]{1,0:T(8,128)(2,1)}, bf16[1024,768]{1,0:T(8,128)(2,1)}, u32[]{:S(2)}, u32[]{:S(2)}) collective-permute-start(bf16[1024,768]{1,0:T(8,128)(2,1)} %collective-permute-done.8.refs_2_), channel_id=1, source_target_pairs={{0,1},{1,0},{2,3},{3,2},{4,5},{5,4},{6,7},{7,6},{8,9},{9,8},{10,11... | collective-permute-start | bytes 4718600 | tf_op jit(solution)/shard_map/ppermute | solution.py:419
  174.8 35.6 %collective-permute-start.11 = (bf16[1024,768]{1,0:T(8,128)(2,1)}, bf16[1024,768]{1,0:T(8,128)(2,1)}, u32[]{:S(2)}, u32[]{:S(2)}) collective-permute-start(bf16[1024,768]{1,0:T(8,128)(2,1)} %collective-permute-done.9.refs_3_), channel_id=1, source_target_pairs={{0,1},{1,0},{2,3},{3,2},{4,5},{5,4},{6,7},{7,6},{8,9},{9,8},{10,11... | collective-permute-start | bytes 4718600 | tf_op jit(solution)/shard_map/ppermute | solution.py:419
  204.3 37.5 %collective-permute-start.16 = (bf16[1024,768]{1,0:T(8,128)(2,1)}, bf16[1024,768]{1,0:T(8,128)(2,1)}, u32[]{:S(2)}, u32[]{:S(2)}) collective-permute-start(bf16[1024,768]{1,0:T(8,128)(2,1)} %collective-permute-done.8.refs_2_), channel_id=1, source_target_pairs={{0,2},{1,3},{2,4},{3,5},{4,6},{5,7},{6,0},{7,1},{8,10},{9,11},{10,... | collective-permute-start | bytes 4718600 | tf_op jit(solution)/shard_map/ppermute | solution.py:419
  206.0 8.4 collective-permute-start.15
  207.1 37.4 %collective-permute-start.17 = (bf16[1024,768]{1,0:T(8,128)(2,1)}, bf16[1024,768]{1,0:T(8,128)(2,1)}, u32[]{:S(2)}, u32[]{:S(2)}) collective-permute-start(bf16[1024,768]{1,0:T(8,128)(2,1)} %collective-permute-done.13.refs_7_), channel_id=1, source_target_pairs={{0,6},{1,7},{2,0},{3,1},{4,2},{5,3},{6,4},{7,5},{8,14},{9,15},{10,... | collective-permute-start | bytes 4718600 | tf_op jit(solution)/shard_map/ppermute | solution.py:419
  210.4 3.8 collective-permute-start.14
  214.2 81.8 %collective-permute-start.32 = (bf16[1024,768]{1,0:T(8,128)(2,1)}, bf16[1024,768]{1,0:T(8,128)(2,1)}, u32[]{:S(2)}, u32[]{:S(2)}) collective-permute-start(bf16[1024,768]{1,0:T(8,128)(2,1)} %copy-done.8), channel_id=1, source_target_pairs={{0,1},{1,0},{2,3},{3,2},{4,5},{5,4},{6,7},{7,6},{8,9},{9,8},{10,11... | collective-permute-start | bytes 4718600 | tf_op jit(solution)/shard_map/ppermute | solution.py:419
  214.5 82.0 %collective-permute-start.38 = (bf16[1024,768]{1,0:T(8,128)(2,1)}, bf16[1024,768]{1,0:T(8,128)(2,1)}, u32[]{:S(2)}, u32[]{:S(2)}) collective-permute-start(bf16[1024,768]{1,0:T(8,128)(2,1)} %copy-done.8), channel_id=1, source_target_pairs={{0,2},{1,3},{2,4},{3,5},{4,6},{5,7},{6,0},{7,1},{8,10},{9,11},{10,... | collective-permute-start | bytes 4718600 | tf_op jit(solution)/shard_map/ppermute | solution.py:419
  241.9 54.8 %collective-permute-start.39 = (bf16[1024,768]{1,0:T(8,128)(2,1)}, bf16[1024,768]{1,0:T(8,128)(2,1)}, u32[]{:S(2)}, u32[]{:S(2)}) collective-permute-start(bf16[1024,768]{1,0:T(8,128)(2,1)} %copy-done.11), channel_id=1, source_target_pairs={{0,6},{1,7},{2,0},{3,1},{4,2},{5,3},{6,4},{7,5},{8,14},{9,15},{10,... | collective-permute-start | bytes 4718600 | tf_op jit(solution)/shard_map/ppermute | solution.py:419
  244.5 52.5 %collective-permute-start.18 = (bf16[1024,768]{1,0:T(8,128)(2,1)}, bf16[1024,768]{1,0:T(8,128)(2,1)}, u32[]{:S(2)}, u32[]{:S(2)}) collective-permute-start(bf16[1024,768]{1,0:T(8,128)(2,1)} %collective-permute-done.16.refs_10_), channel_id=1, source_target_pairs={{0,1},{1,0},{2,3},{3,2},{4,5},{5,4},{6,7},{7,6},{8,9},{9,8},{10,11... | collective-permute-start | bytes 4718600 | tf_op jit(solution)/shard_map/ppermute | solution.py:419
  246.8 50.4 %collective-permute-start.19 = (bf16[1024,768]{1,0:T(8,128)(2,1)}, bf16[1024,768]{1,0:T(8,128)(2,1)}, u32[]{:S(2)}, u32[]{:S(2)}) collective-permute-start(bf16[1024,768]{1,0:T(8,128)(2,1)} %collective-permute-done.17.refs_11_), channel_id=1, source_target_pairs={{0,1},{1,0},{2,3},{3,2},{4,5},{5,4},{6,7},{7,6},{8,9},{9,8},{10,11... | collective-permute-start | bytes 4718600 | tf_op jit(solution)/shard_map/ppermute | solution.py:419
  296.1 77.9 %collective-permute-start.37 = (bf16[1024,768]{1,0:T(8,128)(2,1)}, bf16[1024,768]{1,0:T(8,128)(2,1)}, u32[]{:S(2)}, u32[]{:S(2)}) collective-permute-start(bf16[1024,768]{1,0:T(8,128)(2,1)} %copy-done.11), channel_id=1, source_target_pairs={{0,1},{1,0},{2,3},{3,2},{4,5},{5,4},{6,7},{7,6},{8,9},{9,8},{10,11... | collective-permute-start | bytes 4718600 | tf_op jit(solution)/shard_map/ppermute | solution.py:419
  296.5 77.4 %collective-permute-start.33 = (bf16[1024,768]{1,0:T(8,128)(2,1)}, bf16[1024,768]{1,0:T(8,128)(2,1)}, u32[]{:S(2)}, u32[]{:S(2)}) collective-permute-start(bf16[1024,768]{1,0:T(8,128)(2,1)} %copy-done.9), channel_id=1, source_target_pairs={{0,1},{1,0},{2,3},{3,2},{4,5},{5,4},{6,7},{7,6},{8,9},{9,8},{10,11... | collective-permute-start | bytes 4718600 | tf_op jit(solution)/shard_map/ppermute | solution.py:419
  296.7 77.3 %collective-permute-start.36 = (bf16[1024,768]{1,0:T(8,128)(2,1)}, bf16[1024,768]{1,0:T(8,128)(2,1)}, u32[]{:S(2)}, u32[]{:S(2)}) collective-permute-start(bf16[1024,768]{1,0:T(8,128)(2,1)} %copy-done.10), channel_id=1, source_target_pairs={{0,1},{1,0},{2,3},{3,2},{4,5},{5,4},{6,7},{7,6},{8,9},{9,8},{10,11... | collective-permute-start | bytes 4718600 | tf_op jit(solution)/shard_map/ppermute | solution.py:419
  297.0 77.0 %collective-permute-start.40 = (bf16[1024,768]{1,0:T(8,128)(2,1)}, bf16[1024,768]{1,0:T(8,128)(2,1)}, u32[]{:S(2)}, u32[]{:S(2)}) collective-permute-start(bf16[1024,768]{1,0:T(8,128)(2,1)} %collective-permute-done.38.refs_10_), channel_id=1, source_target_pairs={{0,1},{1,0},{2,3},{3,2},{4,5},{5,4},{6,7},{7,6},{8,9},{9,8},{10,11... | collective-permute-start | bytes 4718600 | tf_op jit(solution)/shard_map/ppermute | solution.py:419
  297.2 76.8 %collective-permute-start.41 = (bf16[1024,768]{1,0:T(8,128)(2,1)}, bf16[1024,768]{1,0:T(8,128)(2,1)}, u32[]{:S(2)}, u32[]{:S(2)}) collective-permute-start(bf16[1024,768]{1,0:T(8,128)(2,1)} %collective-permute-done.39.refs_11_), channel_id=1, source_target_pairs={{0,1},{1,0},{2,3},{3,2},{4,5},{5,4},{6,7},{7,6},{8,9},{9,8},{10,11... | collective-permute-start | bytes 4718600 | tf_op jit(solution)/shard_map/ppermute | solution.py:419
  479.2 435.5 %reduce-scatter.5.cloned.1.call-start = ((), (), s32[]{:S(2)}) async-start(), calls=%async_computation.5 | async-start | bytes 16220160 | tf_op jit(solution)/shard_map/reduce_scatter | solution.py:471
  582.7 157.8 %copy-start.7 = (f32[16,2,2048]{2,1,0:T(2,128)S(1)}, f32[16,2,2048]{2,1,0:T(2,128)}, u32[]{:S(2)}) copy-start(f32[16,2,2048]{2,1,0:T(2,128)} %get-tuple-element.51) | copy-start | bytes 786436
  582.7 286.5 %copy-start.12 = (bf16[1,640,768]{2,1,0:T(8,128)(2,1)S(1)}, bf16[1,640,768]{2,1,0:T(8,128)(2,1)}, u32[]{:S(2)}) copy-start(bf16[1,640,768]{2,1,0:T(8,128)(2,1)} %get-tuple-element.82) | copy-start | bytes 2949124
  582.8 23.6 %collective-permute-start.21 = (bf16[1,640,768]{2,1,0:T(8,128)(2,1)}, bf16[1,640,768]{2,1,0:T(8,128)(2,1)S(1)}, u32[]{:S(2)}, u32[]{:S(2)}) collective-permute-start(bf16[1,640,768]{2,1,0:T(8,128)(2,1)} %get-tuple-element.61), channel_id=1, source_target_pairs={{0,6},{1,7},{2,0},{3,1},{4,2},{5,3},{6,4},{7,5},{8,14},{9,15},{10,... | collective-permute-start | bytes 2949128 | tf_op jit(solution)/shard_map/ppermute | solution.py:419
  585.2 25.4 %collective-permute-start.23 = (bf16[1,640,768]{2,1,0:T(8,128)(2,1)}, bf16[1,640,768]{2,1,0:T(8,128)(2,1)S(1)}, u32[]{:S(2)}, u32[]{:S(2)}) collective-permute-start(bf16[1,640,768]{2,1,0:T(8,128)(2,1)} %get-tuple-element.63), channel_id=1, source_target_pairs={{0,2},{1,3},{2,4},{3,5},{4,6},{5,7},{6,0},{7,1},{8,10},{9,11},{10,... | collective-permute-start | bytes 2949128 | tf_op jit(solution)/shard_map/ppermute | solution.py:419
  585.2 42.2 %collective-permute-start.27 = (bf16[1,640,768]{2,1,0:T(8,128)(2,1)}, bf16[1,640,768]{2,1,0:T(8,128)(2,1)S(1)}, u32[]{:S(2)}, u32[]{:S(2)}) collective-permute-start(bf16[1,640,768]{2,1,0:T(8,128)(2,1)} %get-tuple-element.67), channel_id=1, source_target_pairs={{0,6},{1,7},{2,0},{3,1},{4,2},{5,3},{6,4},{7,5},{8,14},{9,15},{10,... | collective-permute-start | bytes 2949128 | tf_op jit(solution)/shard_map/ppermute | solution.py:419
  587.9 42.9 %collective-permute-start.28 = (bf16[1,640,768]{2,1,0:T(8,128)(2,1)}, bf16[1,640,768]{2,1,0:T(8,128)(2,1)S(1)}, u32[]{:S(2)}, u32[]{:S(2)}) collective-permute-start(bf16[1,640,768]{2,1,0:T(8,128)(2,1)} %get-tuple-element.68), channel_id=1, source_target_pairs={{0,2},{1,3},{2,4},{3,5},{4,6},{5,7},{6,0},{7,1},{8,10},{9,11},{10,... | collective-permute-start | bytes 2949128 | tf_op jit(solution)/shard_map/ppermute | solution.py:419
  587.9 44.7 %collective-permute-start.42 = (bf16[1,640,768]{2,1,0:T(8,128)(2,1)}, bf16[1,640,768]{2,1,0:T(8,128)(2,1)S(1)}, u32[]{:S(2)}, u32[]{:S(2)}) collective-permute-start(bf16[1,640,768]{2,1,0:T(8,128)(2,1)} %get-tuple-element.76), channel_id=1, source_target_pairs={{0,1},{1,0},{2,3},{3,2},{4,5},{5,4},{6,7},{7,6},{8,9},{9,8},{10,11... | collective-permute-start | bytes 2949128 | tf_op jit(solution)/shard_map/ppermute | solution.py:419
  607.3 41.3 %collective-permute-start.43 = (bf16[1,640,768]{2,1,0:T(8,128)(2,1)}, bf16[1,640,768]{2,1,0:T(8,128)(2,1)S(1)}, u32[]{:S(2)}, u32[]{:S(2)}) collective-permute-start(bf16[1,640,768]{2,1,0:T(8,128)(2,1)} %get-tuple-element.77), channel_id=1, source_target_pairs={{0,6},{1,7},{2,0},{3,1},{4,2},{5,3},{6,4},{7,5},{8,14},{9,15},{10,... | collective-permute-start | bytes 2949128 | tf_op jit(solution)/shard_map/ppermute | solution.py:419
  610.6 127.6 %copy-start.16 = (bf16[1,640,768]{2,1,0:T(8,128)(2,1)}, bf16[1,640,768]{2,1,0:T(8,128)(2,1)S(1)}, u32[]{:S(2)}) copy-start(bf16[1,640,768]{2,1,0:T(8,128)(2,1)S(1)} %collective-permute-done.23.refs_4_) | copy-start | bytes 2949124
  610.6 40.0 %collective-permute-start.49 = (bf16[1,640,768]{2,1,0:T(8,128)(2,1)}, bf16[1,640,768]{2,1,0:T(8,128)(2,1)S(1)}, u32[]{:S(2)}, u32[]{:S(2)}) collective-permute-start(bf16[1,640,768]{2,1,0:T(8,128)(2,1)} %get-tuple-element.84), channel_id=1, source_target_pairs={{0,1},{1,0},{2,3},{3,2},{4,5},{5,4},{6,7},{7,6},{8,9},{9,8},{10,11... | collective-permute-start | bytes 2949128 | tf_op jit(solution)/shard_map/ppermute | solution.py:419
  627.5 110.8 %copy-start.17 = (bf16[1,640,768]{2,1,0:T(8,128)(2,1)}, bf16[1,640,768]{2,1,0:T(8,128)(2,1)S(1)}, u32[]{:S(2)}) copy-start(bf16[1,640,768]{2,1,0:T(8,128)(2,1)S(1)} %collective-permute-done.27.refs_8_) | copy-start | bytes 2949124
  627.5 42.1 %collective-permute-start.50 = (bf16[1,640,768]{2,1,0:T(8,128)(2,1)}, bf16[1,640,768]{2,1,0:T(8,128)(2,1)S(1)}, u32[]{:S(2)}, u32[]{:S(2)}) collective-permute-start(bf16[1,640,768]{2,1,0:T(8,128)(2,1)} %get-tuple-element.85), channel_id=1, source_target_pairs={{0,6},{1,7},{2,0},{3,1},{4,2},{5,3},{6,4},{7,5},{8,14},{9,15},{10,... | collective-permute-start | bytes 2949128 | tf_op jit(solution)/shard_map/ppermute | solution.py:419
  630.8 60.9 %collective-permute-start.51 = (bf16[1,640,768]{2,1,0:T(8,128)(2,1)}, bf16[1,640,768]{2,1,0:T(8,128)(2,1)S(1)}, u32[]{:S(2)}, u32[]{:S(2)}) collective-permute-start(bf16[1,640,768]{2,1,0:T(8,128)(2,1)} %get-tuple-element.86), channel_id=1, source_target_pairs={{0,7},{1,6},{2,1},{3,0},{4,3},{5,2},{6,5},{7,4},{8,15},{9,14},{10,... | collective-permute-start | bytes 2949128 | tf_op jit(solution)/shard_map/ppermute | solution.py:419
  632.7 101.3 %collective-permute-start.52 = (bf16[1,640,768]{2,1,0:T(8,128)(2,1)}, bf16[1,640,768]{2,1,0:T(8,128)(2,1)S(1)}, u32[]{:S(2)}, u32[]{:S(2)}) collective-permute-start(bf16[1,640,768]{2,1,0:T(8,128)(2,1)} %get-tuple-element.87), channel_id=1, source_target_pairs={{0,2},{1,3},{2,4},{3,5},{4,6},{5,7},{6,0},{7,1},{8,10},{9,11},{10,... | collective-permute-start | bytes 2949128 | tf_op jit(solution)/shard_map/ppermute | solution.py:419
  648.6 88.4 %collective-permute-start.53 = (bf16[1,640,768]{2,1,0:T(8,128)(2,1)}, bf16[1,640,768]{2,1,0:T(8,128)(2,1)S(1)}, u32[]{:S(2)}, u32[]{:S(2)}) collective-permute-start(bf16[1,640,768]{2,1,0:T(8,128)(2,1)} %get-tuple-element.88), channel_id=1, source_target_pairs={{0,3},{1,2},{2,5},{3,4},{4,7},{5,6},{6,1},{7,0},{8,11},{9,10},{10,... | collective-permute-start | bytes 2949128 | tf_op jit(solution)/shard_map/ppermute | solution.py:419
  650.6 86.3 %collective-permute-start.54 = (bf16[1,640,768]{2,1,0:T(8,128)(2,1)}, bf16[1,640,768]{2,1,0:T(8,128)(2,1)S(1)}, u32[]{:S(2)}, u32[]{:S(2)}) collective-permute-start(bf16[1,640,768]{2,1,0:T(8,128)(2,1)} %get-tuple-element.89), channel_id=1, source_target_pairs={{0,4},{1,5},{2,6},{3,7},{4,0},{5,1},{6,2},{7,3},{8,12},{9,13},{10,... | collective-permute-start | bytes 2949128 | tf_op jit(solution)/shard_map/ppermute | solution.py:419
  669.6 68.6 %collective-permute-start.55 = (bf16[1,640,768]{2,1,0:T(8,128)(2,1)}, bf16[1,640,768]{2,1,0:T(8,128)(2,1)S(1)}, u32[]{:S(2)}, u32[]{:S(2)}) collective-permute-start(bf16[1,640,768]{2,1,0:T(8,128)(2,1)} %get-tuple-element.90), channel_id=1, source_target_pairs={{0,5},{1,4},{2,7},{3,6},{4,1},{5,0},{6,3},{7,2},{8,13},{9,12},{10,... | collective-permute-start | bytes 2949128 | tf_op jit(solution)/shard_map/ppermute | solution.py:419
  691.7 49.7 %collective-permute-start.20 = (bf16[2,640,768]{2,1,0:T(8,128)(2,1)S(1)}, bf16[2,640,768]{2,1,0:T(8,128)(2,1)}, u32[]{:S(2)}, u32[]{:S(2)}) collective-permute-start(bf16[2,640,768]{2,1,0:T(8,128)(2,1)S(1)} %copy-done.2), channel_id=1, source_target_pairs={{0,1},{1,0},{2,3},{3,2},{4,5},{5,4},{6,7},{7,6},{8,9},{9,8},{10,11... | collective-permute-start | bytes 5898248 | tf_op jit(solution)/shard_map/ppermute | solution.py:419
  734.0 129.8 %collective-permute-start.22 = (bf16[2,640,768]{2,1,0:T(8,128)(2,1)}, bf16[2,640,768]{2,1,0:T(8,128)(2,1)}, u32[]{:S(2)}, u32[]{:S(2)}) collective-permute-start(bf16[2,640,768]{2,1,0:T(8,128)(2,1)} %get-tuple-element.62), channel_id=1, source_target_pairs={{0,7},{1,6},{2,1},{3,0},{4,3},{5,2},{6,5},{7,4},{8,15},{9,14},{10,... | collective-permute-start | bytes 5898248 | tf_op jit(solution)/shard_map/ppermute | solution.py:419
  736.9 130.3 %collective-permute-start.24 = (bf16[2,640,768]{2,1,0:T(8,128)(2,1)}, bf16[2,640,768]{2,1,0:T(8,128)(2,1)}, u32[]{:S(2)}, u32[]{:S(2)}) collective-permute-start(bf16[2,640,768]{2,1,0:T(8,128)(2,1)} %get-tuple-element.64), channel_id=1, source_target_pairs={{0,3},{1,2},{2,5},{3,4},{4,7},{5,6},{6,1},{7,0},{8,11},{9,10},{10,... | collective-permute-start | bytes 5898248 | tf_op jit(solution)/shard_map/ppermute | solution.py:419
  737.0 130.3 %collective-permute-start.25 = (bf16[2,640,768]{2,1,0:T(8,128)(2,1)}, bf16[2,640,768]{2,1,0:T(8,128)(2,1)}, u32[]{:S(2)}, u32[]{:S(2)}) collective-permute-start(bf16[2,640,768]{2,1,0:T(8,128)(2,1)} %get-tuple-element.65), channel_id=1, source_target_pairs={{0,4},{1,5},{2,6},{3,7},{4,0},{5,1},{6,2},{7,3},{8,12},{9,13},{10,... | collective-permute-start | bytes 5898248 | tf_op jit(solution)/shard_map/ppermute | solution.py:419
  738.3 130.8 %collective-permute-start.26 = (bf16[2,640,768]{2,1,0:T(8,128)(2,1)}, bf16[2,640,768]{2,1,0:T(8,128)(2,1)}, u32[]{:S(2)}, u32[]{:S(2)}) collective-permute-start(bf16[2,640,768]{2,1,0:T(8,128)(2,1)} %get-tuple-element.66), channel_id=1, source_target_pairs={{0,5},{1,4},{2,7},{3,6},{4,1},{5,0},{6,3},{7,2},{8,13},{9,12},{10,... | collective-permute-start | bytes 5898248 | tf_op jit(solution)/shard_map/ppermute | solution.py:419
  741.4 185.5 %collective-permute-start.44 = (bf16[1,640,768]{2,1,0:T(8,128)(2,1)}, bf16[1,640,768]{2,1,0:T(8,128)(2,1)}, u32[]{:S(2)}, u32[]{:S(2)}) collective-permute-start(bf16[1,640,768]{2,1,0:T(8,128)(2,1)} %get-tuple-element.78), channel_id=1, source_target_pairs={{0,7},{1,6},{2,1},{3,0},{4,3},{5,2},{6,5},{7,4},{8,15},{9,14},{10,... | collective-permute-start | bytes 2949128 | tf_op jit(solution)/shard_map/ppermute | solution.py:419
  863.7 63.2 %collective-permute-start.45 = (bf16[1,640,768]{2,1,0:T(8,128)(2,1)}, bf16[1,640,768]{2,1,0:T(8,128)(2,1)}, u32[]{:S(2)}, u32[]{:S(2)}) collective-permute-start(bf16[1,640,768]{2,1,0:T(8,128)(2,1)} %get-tuple-element.79), channel_id=1, source_target_pairs={{0,2},{1,3},{2,4},{3,5},{4,6},{5,7},{6,0},{7,1},{8,10},{9,11},{10,... | collective-permute-start | bytes 2949128 | tf_op jit(solution)/shard_map/ppermute | solution.py:419
  867.3 59.7 %collective-permute-start.46 = (bf16[1,640,768]{2,1,0:T(8,128)(2,1)}, bf16[1,640,768]{2,1,0:T(8,128)(2,1)}, u32[]{:S(2)}, u32[]{:S(2)}) collective-permute-start(bf16[1,640,768]{2,1,0:T(8,128)(2,1)} %get-tuple-element.80), channel_id=1, source_target_pairs={{0,3},{1,2},{2,5},{3,4},{4,7},{5,6},{6,1},{7,0},{8,11},{9,10},{10,... | collective-permute-start | bytes 2949128 | tf_op jit(solution)/shard_map/ppermute | solution.py:419
  867.3 66.2 %collective-permute-start.47 = (bf16[1,640,768]{2,1,0:T(8,128)(2,1)}, bf16[1,640,768]{2,1,0:T(8,128)(2,1)}, u32[]{:S(2)}, u32[]{:S(2)}) collective-permute-start(bf16[1,640,768]{2,1,0:T(8,128)(2,1)} %get-tuple-element.81), channel_id=1, source_target_pairs={{0,4},{1,5},{2,6},{3,7},{4,0},{5,1},{6,2},{7,3},{8,12},{9,13},{10,... | collective-permute-start | bytes 2949128 | tf_op jit(solution)/shard_map/ppermute | solution.py:419
  869.2 85.4 %collective-permute-start.48 = (bf16[1,640,768]{2,1,0:T(8,128)(2,1)S(1)}, bf16[1,640,768]{2,1,0:T(8,128)(2,1)}, u32[]{:S(2)}, u32[]{:S(2)}) collective-permute-start(bf16[1,640,768]{2,1,0:T(8,128)(2,1)S(1)} %copy-done.12), channel_id=1, source_target_pairs={{0,5},{1,4},{2,7},{3,6},{4,1},{5,0},{6,3},{7,2},{8,13},{9,12},{10,... | collective-permute-start | bytes 2949128 | tf_op jit(solution)/shard_map/ppermute | solution.py:419
  (22 other events, 853.5 us)
Sparse Core Ops, SparseCore 0:
  12.1 68.4 all-gather.2
  82.2 65.4 all-gather.4
  479.4 117.6 reduce-scatter.2
  599.3 114.8 reduce-scatter.4
